TPU v7x, 8 devices: a whole 2x2x1 slice. The times are simulated.
8 devices in a mesh: batch: 2 (over z, y), col: 4 (over x, core).
Axes of the slice: x: 2, y: 2, z: 1, core: 2. Of those that a mesh axis runs over, the one named last changes fastest.
Arguments:
- lower: bfloat16 [4096, 2048], P('batch', 'col'), parts along dimension 0
- rhs: bfloat16 [4096, 32768], P('batch', 'col'), parts along dimension 0
Outputs:
- output: bfloat16 [4096, 32768], P('batch', 'col'), parts along dimension 0
There are 2 independent parts. A program takes and returns all parts, laid end to end along the dimension named above; each array names one.
All inputs are finite; a program needn't handle non-finite values.
Results may differ from a plain program's by a relative error of at most 0.001.
Values are sent between devices in bfloat16 or wider.
A program may use at most 1 GiB of HBM per device.

v0:
```python
import jax
import jax.numpy as jnp
from jax import lax
from jax.sharding import PartitionSpec as P

BLOCK_SIZE = 256


def solution(mesh):
    group_size = mesh.shape["col"]

    def local_product(l_cols, b_cols):
        mat_order, local_width = l_cols.shape
        per_dev = local_width // BLOCK_SIZE
        super_width = group_size * BLOCK_SIZE
        pieces = [l_cols[panel_idx * super_width:, panel_idx * BLOCK_SIZE:(panel_idx + 1) * BLOCK_SIZE] for panel_idx in range(per_dev)]
        packed = jnp.concatenate(pieces, axis=0)
        gathered = lax.all_gather(packed, "col")
        col_bands = []
        offset = 0
        for panel_idx in range(per_dev):
            band_rows = mat_order - panel_idx * super_width
            panel_band = gathered[:, offset:offset + band_rows, :]
            offset = offset + band_rows
            panel_band = jnp.transpose(panel_band, (1, 0, 2)).reshape(band_rows, super_width)
            col_bands.append(jnp.pad(panel_band, ((panel_idx * super_width, 0), (0, 0))))
        natural = jnp.concatenate(col_bands, axis=1)
        out_rows = []
        for row_idx in range(mat_order // BLOCK_SIZE):
            row_end = (row_idx + 1) * BLOCK_SIZE
            strip = natural[row_idx * BLOCK_SIZE:row_end, :row_end]
            block_out = jnp.dot(strip, b_cols[:row_end], preferred_element_type=jnp.float32)
            out_rows.append(block_out.astype(jnp.bfloat16))
        return jnp.concatenate(out_rows, axis=0)

    return jax.shard_map(local_product, mesh=mesh, in_specs=(P("batch", "col"), P("batch", "col")), out_specs=P("batch", "col"), check_vma=False)
```

profile of v0, /device:TPU:0, one launch (start us, length us, event | category | flops | bytes accessed | tf_op | source)
XLA Modules:
  0.0 178.4 jit_solution(7478795677490517045)
XLA Ops:
  6.5 0.0 all-gather.3.cloned.1.call-start
  6.5 1.1 slice.61
  7.6 1.3 slice.60
  8.9 1.2 pad_maximum_fusion
  10.2 0.0 all-gather.3.cloned.1.call-update
  10.2 46.6 %all-gather.3.cloned.1.call-done = bf16[12288,256]{1,0:T(8,128)(2,1)} async-done(((bf16[3072,256]{1,0:T(8,128)(2,1)}), bf16[12288,256]{1,0:T(8,128)(2,1)}) %all-gather.3.cloned.1.call-update) | async-done | bytes 6291472 | tf_op jit(solution)/shard_map/all_gather | solution.py:18
  56.8 1.7 slice_bitcast_fusion.1
  58.5 2.5 %slice_bitcast_fusion = bf16[2048,4,256]{2,0,1:T(8,128)(2,1)S(1)} fusion(bf16[4,3072,256]{2,1,0:T(8,128)(2,1)} %bitcast.16), kind=kLoop, calls=%fused_computation.30 | loop fusion | bytes 8388608 | tf_op jit(solution)/shard_map/transpose | solution.py:25
  61.0 0.0 copy-start
  61.0 2.0 %copy-done = bf16[2048,4,256]{2,0,1:T(8,128)(2,1)} copy-done((bf16[2048,4,256]{2,0,1:T(8,128)(2,1)}, bf16[2048,4,256]{2,0,1:T(8,128)(2,1)S(1)}, u32[]{:S(2)}) %copy-start) | copy-done | bytes 4194328
  63.0 0.0 slice-start
  63.0 6.4 %copy.3 = bf16[2048,4,256]{0,2,1:T(8,128)(2,1)} copy(bf16[2048,4,256]{2,0,1:T(8,128)(2,1)} %copy-done) | data formatting | bytes 8388608 | tf_op jit(solution)/shard_map/transpose | solution.py:25
  69.4 2.5 %copy.5 = bf16[1024,4,256]{0,2,1:T(8,128)(2,1)} copy(bf16[1024,4,256]{2,0,1:T(8,128)(2,1)S(1)} %slice_bitcast_fusion.1) | data formatting | bytes 4194304 | tf_op jit(solution)/shard_map/transpose | solution.py:25
  71.9 0.0 slice-done
  71.9 0.2 copy.4
  72.1 4.2 %fusion.44 = bf16[2048,2048]{0,1:T(8,128)(2,1)S(1)} fusion(bf16[1024,1024]{0,1:T(8,128)(2,1)} %bitcast.14, bf16[2048,1024]{0,1:T(8,128)(2,1)} %bitcast.10), kind=kLoop, calls=%fused_computation.28 | loop fusion | flops 25165824 | bytes 14680064 | tf_op jit(solution)/shard_map/concatenate | solution.py:27
  76.3 0.0 copy-start.1
  76.3 8.6 %fusion.28 = bf16[2048,8192]{1,0:T(8,128)(2,1)} fusion(bf16[2048,8192]{1,0:T(8,128)(2,1)} %param.3, bf16[2048,1024]{0,1:T(8,128)(2,1)} %bitcast.11), kind=kOutput, calls=%fused_computation.22 | convolution fusion | flops 1075838976 | bytes 8519680 | tf_op jit(solution)/shard_map/dot_general | solution.py:32
  84.8 7.9 %fusion.23 = bf16[2048,8192]{1,0:T(8,128)(2,1)} fusion(bf16[2048,8192]{1,0:T(8,128)(2,1)} %fusion.28, bf16[2048,8192]{1,0:T(8,128)(2,1)} %param.3, bf16[2048,1024]{0,1:T(8,128)(2,1)} %bitcast.12), kind=kOutput, calls=%fused_computation.17 | convolution fusion | flops 2149580800 | bytes 12845056 | tf_op jit(solution)/shard_map/dot_general | solution.py:32
  92.7 10.2 %fusion.41 = bf16[2048,8192]{1,0:T(8,128)(2,1)} fusion(bf16[2048,8192]{1,0:T(8,128)(2,1)} %fusion.23, bf16[2048,8192]{1,0:T(8,128)(2,1)} %param.3, bf16[2048,1024]{0,1:T(8,128)(2,1)} %bitcast.13), kind=kOutput, calls=%fused_computation.27 | convolution fusion | flops 3223322624 | bytes 17170432 | tf_op jit(solution)/shard_map/dot_general | solution.py:32
  102.9 12.4 %fusion.38 = bf16[2048,8192]{1,0:T(8,128)(2,1)} fusion(bf16[2048,8192]{1,0:T(8,128)(2,1)} %fusion.41, bf16[256,1024]{0,1:T(8,128)(2,1)S(1)} %bitcast.17, bf16[2048,8192]{1,0:T(8,128)(2,1)} %param.3), kind=kOutput, calls=%fused_computation.26 | convolution fusion | flops 4297064448 | bytes 21495808 | tf_op jit(solution)/shard_map/dot_general | solution.py:32
  115.3 0.0 copy-done.1
  115.3 11.3 %fusion.35 = bf16[2048,8192]{1,0:T(8,128)(2,1)} fusion(bf16[2048,8192]{1,0:T(8,128)(2,1)} %fusion.38, bf16[2048,8192]{1,0:T(8,128)(2,1)} %param.3, bf16[2048,2048]{0,1:T(8,128)(2,1)S(1)} %fusion.44), kind=kOutput, calls=%fused_computation.25 | convolution fusion | flops 5370806272 | bytes 25821184 | tf_op jit(solution)/shard_map/dot_general | solution.py:32
  126.6 13.2 %fusion.32 = bf16[2048,8192]{1,0:T(8,128)(2,1)} fusion(bf16[2048,8192]{1,0:T(8,128)(2,1)} %fusion.35, bf16[2048,8192]{1,0:T(8,128)(2,1)} %param.3, bf16[2048,2048]{0,1:T(8,128)(2,1)} %copy-done.1), kind=kOutput, calls=%fused_computation.24 | convolution fusion | flops 6444548096 | bytes 30146560 | tf_op jit(solution)/shard_map/dot_general | solution.py:32
  139.8 15.0 %fusion.29 = bf16[2048,8192]{1,0:T(8,128)(2,1)} fusion(bf16[2048,8192]{1,0:T(8,128)(2,1)} %fusion.32, bf16[2048,8192]{1,0:T(8,128)(2,1)} %param.3, bf16[2048,2048]{0,1:T(8,128)(2,1)} %copy-done.1), kind=kOutput, calls=%fused_computation.23 | convolution fusion | flops 7518289920 | bytes 34471936 | tf_op jit(solution)/shard_map/dot_general | solution.py:32
  154.8 16.8 %fusion.27 = bf16[2048,8192]{1,0:T(8,128)(2,1)} fusion(bf16[2048,8192]{1,0:T(8,128)(2,1)} %fusion.29, bf16[2048,8192]{1,0:T(8,128)(2,1)} %param.3, bf16[2048,2048]{0,1:T(8,128)(2,1)} %copy-done.1), kind=kOutput, calls=%fused_computation.20 | convolution fusion | flops 8592031744 | bytes 38797312 | tf_op jit(solution)/shard_map/dot_general | solution.py:32
Async XLA Ops:
  6.5 50.2 %all-gather.3.cloned.1.call-start = ((), (), s32[]{:S(2)}) async-start(), calls=%async_computation | async-start | bytes 7864320 | tf_op jit(solution)/shard_map/all_gather | solution.py:18
  61.0 2.0 %copy-start = (bf16[2048,4,256]{2,0,1:T(8,128)(2,1)}, bf16[2048,4,256]{2,0,1:T(8,128)(2,1)S(1)}, u32[]{:S(2)}) copy-start(bf16[2048,4,256]{2,0,1:T(8,128)(2,1)S(1)} %slice_bitcast_fusion) | copy-start | bytes 12582916
  63.0 8.9 %slice-start = ((bf16[2048,4,256]{2,0,1:T(8,128)(2,1)}), bf16[256,4,256]{2,0,1:T(8,128)(2,1)S(1)}, s32[]{:S(2)}) async-start(bf16[2048,4,256]{2,0,1:T(8,128)(2,1)} %copy-done), calls=%async_computation.1 | async-start | bytes 1048576 | tf_op jit(solution)/shard_map/slice | solution.py:31
  76.3 39.1 %copy-start.1 = (bf16[2048,2048]{0,1:T(8,128)(2,1)}, bf16[2048,2048]{0,1:T(8,128)(2,1)S(1)}, u32[]{:S(2)}) copy-start(bf16[2048,2048]{0,1:T(8,128)(2,1)S(1)} %fusion.44) | copy-start | bytes 25165828
Sparse Core Ops, SparseCore 0:
  10.3 46.4 all-gather.2
where the time goes:
time: 179 us; the launch traced here: 178 us
  matrix products  95.3 us (53%)
  waiting for transfers between devices  46.6 us (26%)
  local copies, waits for them, and re-layouts  17.7 us (10%)
  between operations  13.4 us (7%)
  other arithmetic  5.41 us (3%)
    dot_general x8, matrix products, local_product(): jnp.dot(strip, b_cols[:row_end], preferred_element_type=jnp.float32)  95.3 us
    all_gather x1, waiting for transfers between devices, local_product(): gathered = lax.all_gather(packed, 'col')  46.6 us
    transpose x4, local copies, waits for them, and re-layouts, local_product(): jnp.transpose(panel_band, (1, 0, 2)).reshape(band_rows, super_width)  13.1 us
    concatenate x1, other arithmetic, local_product(): natural = jnp.concatenate(col_bands, axis=1)  4.17 us
  transfers between devices with their start and end apart: 1, of which 1 were waited for; matrix products, arithmetic and copies ran while one was open for 0% of the time, Pallas kernels for 0%

commit v1 on v0

v1 whole, which is shorter than its diff:
```python
import jax
import jax.numpy as jnp
from jax import lax
from jax.experimental import pallas as pl
from jax.experimental.pallas import tpu as pltpu
from jax.sharding import PartitionSpec as P

BLOCK = 256
MESH = pl.DeviceIdType.MESH
MIB = 1024 * 1024
EARLY = 5632
TILE = 512


def when(cond, fn):
    if cond is True:
        fn()
    elif cond is not False:
        pl.when(cond)(fn)


def solution(mesh):
    group = mesh.shape["col"]

    def local_product(l_cols, b_cols):
        order, local_width = l_cols.shape
        width = b_cols.shape[1]
        per_dev = local_width // BLOCK
        n_rows = order // BLOCK
        late = width - EARLY
        n_late = late // TILE
        dtype = b_cols.dtype

        def held(row, owner, t):
            low, high = group * t, group * t + group - 1
            if row >= high:
                return True
            if row < low:
                return False
            return owner + low <= row

        def gather_kernel(l_ref, b_ref, *refs):
            x_refs, l_refs = refs[:n_rows], refs[n_rows:2 * n_rows]
            b_vmem, b_sem, own_sem, x_send, x_recv, p_send, p_recv, f_send, f_recv = refs[2 * n_rows:]
            me = lax.axis_index("col")
            across = lax.rem(me + 2, group)
            partner = me + 1 - 2 * lax.rem(me, 2)
            diagonal = lax.rem(partner + 2, group)

            barrier = pltpu.get_barrier_semaphore()
            for peer in (partner, across):
                pl.semaphore_signal(barrier, inc=1, device_id={"col": peer}, device_id_type=MESH)
            pl.semaphore_wait(barrier, 2)

            def panel(row, owner, t):
                start = pl.multiple_of((owner + group * t) * BLOCK, BLOCK)
                return l_refs[row].at[:, pl.ds(start, BLOCK)]

            def mine(row, t):
                return l_ref.at[pl.ds(row * BLOCK, BLOCK), pl.ds(t * BLOCK, BLOCK)]

            def own_copy(row, t):
                return pltpu.make_async_copy(mine(row, t), panel(row, me, t), own_sem.at[row, t])

            def send(row, t, peer, send_sem, recv_sem):
                return pltpu.make_async_remote_copy(
                    src_ref=mine(row, t), dst_ref=panel(row, me, t), send_sem=send_sem.at[row, t],
                    recv_sem=recv_sem.at[row, t], device_id={"col": peer}, device_id_type=MESH)

            def arrival(row, t, owner, recv_sem):
                dst = panel(row, owner, t)
                return pltpu.make_async_remote_copy(
                    src_ref=dst, dst_ref=dst, send_sem=x_send.at[row, t], recv_sem=recv_sem.at[row, t],
                    device_id={"col": partner}, device_id_type=MESH)

            def forward(row, t):
                block = panel(row, across, t)
                return pltpu.make_async_remote_copy(
                    src_ref=block, dst_ref=block, send_sem=f_send.at[row, t], recv_sem=f_recv.at[row, t],
                    device_id={"col": partner}, device_id_type=MESH)

            def load_b(k):
                rows = pl.ds(k * BLOCK, BLOCK)
                return pltpu.make_async_copy(b_ref.at[rows, pl.ds(0, EARLY)], b_vmem.at[rows, :], b_sem.at[k])

            sequence = list(range(n_rows - 1, -1, -1))
            blocks = [(row, t) for row in sequence for t in range(per_dev)]
            for row, t in blocks:
                when(held(row, me, t), lambda row=row, t=t: send(row, t, across, x_send, x_recv).start())
            for row, t in blocks:
                def start_near(row=row, t=t):
                    send(row, t, partner, p_send, p_recv).start()
                    own_copy(row, t).start()
                when(held(row, me, t), start_near)
            for k in range(n_rows):
                load_b(k).start()

            def relay(row):
                for t in range(per_dev):
                    def step(t=t):
                        arrival(row, t, across, x_recv).wait_recv()
                        forward(row, t).start()
                    when(held(row, across, t), step)

            def multiply(row, first, last, step):
                depth = (row + 1) * BLOCK

                def body(n, carry):
                    cols = pl.ds(pl.multiple_of(n * step, TILE), step)
                    x_refs[row][:, cols] = jnp.dot(
                        l_refs[row][...], b_vmem[pl.ds(0, depth), cols],
                        preferred_element_type=jnp.float32).astype(dtype)
                    return carry

                lax.fori_loop(first, last, body, 0)

            relay(sequence[0])
            for place, row in enumerate(sequence):
                for t in range(per_dev):
                    when(held(row, me, t), lambda t=t: own_copy(row, t).wait())
                    when(held(row, partner, t), lambda t=t: arrival(row, t, partner, p_recv).wait_recv())
                    when(held(row, diagonal, t), lambda t=t: arrival(row, t, diagonal, f_recv).wait_recv())
                if place == 0:
                    for k in range(n_rows):
                        load_b(k).wait()
                step = TILE
                count = EARLY // step
                split = (count * 3) // 4
                multiply(row, 0, split, step)
                if place + 1 < n_rows:
                    relay(sequence[place + 1])
                multiply(row, split, count, step)

            for row, t in blocks:
                def drain(row=row, t=t):
                    send(row, t, across, x_send, x_recv).wait_send()
                    send(row, t, partner, p_send, p_recv).wait_send()
                when(held(row, me, t), drain)
                when(held(row, across, t), lambda row=row, t=t: forward(row, t).wait_send())

        dma = pltpu.SemaphoreType.DMA
        vmem = pl.BlockSpec(memory_space=pltpu.VMEM)
        hbm = pl.BlockSpec(memory_space=pl.ANY)
        gathered = pl.pallas_call(
            gather_kernel,
            out_shape=tuple(pltpu.VMEM((BLOCK, EARLY), dtype) for _ in range(n_rows))
            + tuple(pltpu.VMEM((BLOCK, BLOCK * (i + 1)), dtype) for i in range(n_rows)),
            in_specs=[hbm, hbm],
            out_specs=(vmem,) * (2 * n_rows),
            scratch_shapes=[pltpu.VMEM((order, EARLY), dtype), dma((n_rows,))] + [dma((n_rows, per_dev))] * 7,
            compiler_params=pltpu.CompilerParams(
                collective_id=0, has_side_effects=True, vmem_limit_bytes=27 * MIB),
            name="gather_and_multiply",
        )(l_cols, b_cols)

        def finish_kernel(*refs):
            x_refs, l_refs = refs[:n_rows], refs[n_rows:2 * n_rows]
            b_ref, out_ref, b_vmem, x_vmem, b_sem, x_sem, early_sem = refs[2 * n_rows:]

            def load_b(n):
                return pltpu.make_async_copy(
                    b_ref.at[:, pl.ds(pl.multiple_of(EARLY + n * TILE, TILE), TILE)], b_vmem.at[n], b_sem.at[n])

            def put_early(row):
                return pltpu.make_async_copy(
                    x_refs[row], out_ref.at[pl.ds(row * BLOCK, BLOCK), pl.ds(0, EARLY)], early_sem.at[row])

            def put_late(n):
                return pltpu.make_async_copy(
                    x_vmem.at[n], out_ref.at[:, pl.ds(pl.multiple_of(EARLY + n * TILE, TILE), TILE)], x_sem.at[n])

            for n in range(n_late):
                load_b(n).start()
            for row in range(n_rows):
                put_early(row).start()

            def body(n, carry):
                load_b(n).wait()
                for row in range(n_rows - 1, -1, -1):
                    depth = (row + 1) * BLOCK
                    x_vmem[n, pl.ds(row * BLOCK, BLOCK), :] = jnp.dot(
                        l_refs[row][...], b_vmem[n, pl.ds(0, depth), :],
                        preferred_element_type=jnp.float32).astype(dtype)
                put_late(n).start()
                return carry

            lax.fori_loop(0, n_late, body, 0)
            for n in range(n_late):
                put_late(n).wait()
            for row in range(n_rows):
                put_early(row).wait()

        return pl.pallas_call(
            finish_kernel,
            out_shape=jax.ShapeDtypeStruct((order, width), dtype),
            in_specs=[vmem] * (2 * n_rows) + [hbm],
            out_specs=hbm,
            scratch_shapes=[
                pltpu.VMEM((n_late, order, TILE), dtype), pltpu.VMEM((n_late, order, TILE), dtype),
                dma((n_late,)), dma((n_late,)), dma((n_rows,))],
            compiler_params=pltpu.CompilerParams(vmem_limit_bytes=26 * MIB),
            name="finish",
        )(*gathered, b_cols)

    return jax.shard_map(local_product, mesh=mesh, in_specs=(P("batch", "col"), P("batch", "col")), out_specs=P("batch", "col"), check_vma=False)
```

time: 179 us -> 71.9 us (0.40)
  matrix products: 95.3 us -> 0 us
  Pallas kernels: 0 us -> 71.8 us
  waiting for transfers between devices: 46.6 us -> 0 us
  local copies, waits for them, and re-layouts: 17.7 us -> 0 us
  between operations: 13.4 us -> 0.01 us
  other arithmetic: 5.41 us -> 0 us
    dot_general x8 -> x0, matrix products: 95.3 us -> none  [local_product(): jnp.dot(strip, b_cols[:row_end], preferred_element_type=jnp.float32)]
    pallas_call x0 -> x2, Pallas kernels: none -> 71.8 us  [the longest x1 54.1 us: local_product(): pl.pallas_call(gather_kernel, out_shape=tuple((pltpu.VMEM((BLOCK, EARLY),...]
    all_gather x1 -> x0, waiting for transfers between devices: 46.6 us -> none  [local_product(): gathered = lax.all_gather(packed, 'col')]
    transpose x4 -> x0, local copies, waits for them, and re-layouts: 13.1 us -> none  [local_product(): jnp.transpose(panel_band, (1, 0, 2)).reshape(band_rows, super_width)]
    concatenate x2 -> x0, other arithmetic: 5.41 us -> none  [the longest x1 4.17 us: local_product(): natural = jnp.concatenate(col_bands, axis=1)]
    slice x5 -> x0, local copies, waits for them, and re-layouts: 2.58 us -> none  [the longest x2 2.37 us: local_product(): l_cols[panel_idx * super_width:, panel_idx * BLOCK_SIZE:(panel_idx + 1) *...]
    unnamed x4 -> x0, local copies, waits for them, and re-layouts: 2.01 us -> none
  transfers between devices with their start and end apart: 1 -> 0, of which waited for: 1 -> 0; matrix products, arithmetic and copies ran while one was open for 0% -> 0% of each run, Pallas kernels for 0% -> 0%
where the time goes in v1:
time: 71.9 us
  Pallas kernels  71.8 us (100%)
    pallas_call x1, Pallas kernels, local_product(): pl.pallas_call(gather_kernel, out_shape=tuple((pltpu.VMEM((BLOCK, EARLY),...  54.1 us
    pallas_call x1, Pallas kernels, local_product(): pl.pallas_call(finish_kernel, out_shape=jax.ShapeDtypeStruct((order, widt...  17.7 us

profile of v1, /device:TPU:0, one launch (start us, length us, event | category | flops | bytes accessed | tf_op | source)
XLA Modules:
  0.0 71.9 jit_solution(9297816107371705990)
XLA Ops:
  0.0 54.1 %gather_and_multiply.1 = (bf16[256,5632]{1,0:T(8,128)(2,1)S(1)}, bf16[256,5632]{1,0:T(8,128)(2,1)S(1)}, bf16[256,5632]{1,0:T(8,128)(2,1)S(1)}, bf16[256,5632]{1,...) custom-call(bf16[2048,512]{1,0:T(8,128)(2,1)} %l_ref.1, ...), custom_call_target="tpu_custom_call" | custom-call | tf_op jit(solution)/shard_map/gather_and_multiply/pallas_call | solution.py:144
  54.1 17.7 %finish.1 = bf16[2048,8192]{1,0:T(8,128)(2,1)} custom-call(bf16[256,5632]{1,0:T(8,128)(2,1)S(1)} %get-tuple-element.21.refs_0_, bf16[256,5632]{1,0:T(8,128)(2,1)S(1)} %get-tuple-element.22.refs_1_, bf16[256,5632]{1,0:T(8,128)(2,1)S(1)} %get-tuple-element.23.refs_2_, bf16[256,5632]{1,0:T(8,128)(2,1)S(1)} %get-tuple-element.24.refs_3_, ...), custom_call_target="tpu_custom_call" | custom-call | tf_op jit(solution)/shard_map/finish/pallas_call | solution.py:193

commit v2 on v1

--- a/solution.py
+++ b/solution.py
@@ -83,7 +83,7 @@
                 rows = pl.ds(k * BLOCK, BLOCK)
                 return pltpu.make_async_copy(b_ref.at[rows, pl.ds(0, EARLY)], b_vmem.at[rows, :], b_sem.at[k])
 
-            sequence = list(range(n_rows - 1, -1, -1))
+            sequence = [3, 7, 6, 5, 4, 2, 1, 0]
             blocks = [(row, t) for row in sequence for t in range(per_dev)]
             for row, t in blocks:
                 when(held(row, me, t), lambda row=row, t=t: send(row, t, across, x_send, x_recv).start())
@@ -102,34 +102,27 @@
                         forward(row, t).start()
                     when(held(row, across, t), step)
 
-            def multiply(row, first, last, step):
+            def multiply(row, start, stop):
                 depth = (row + 1) * BLOCK
-
-                def body(n, carry):
-                    cols = pl.ds(pl.multiple_of(n * step, TILE), step)
-                    x_refs[row][:, cols] = jnp.dot(
-                        l_refs[row][...], b_vmem[pl.ds(0, depth), cols],
-                        preferred_element_type=jnp.float32).astype(dtype)
-                    return carry
-
-                lax.fori_loop(first, last, body, 0)
+                x_refs[row][:, start:stop] = jnp.dot(
+                    l_refs[row][...], b_vmem[:depth, start:stop],
+                    preferred_element_type=jnp.float32).astype(dtype)
 
             relay(sequence[0])
+            loaded = 0
             for place, row in enumerate(sequence):
                 for t in range(per_dev):
                     when(held(row, me, t), lambda t=t: own_copy(row, t).wait())
                     when(held(row, partner, t), lambda t=t: arrival(row, t, partner, p_recv).wait_recv())
                     when(held(row, diagonal, t), lambda t=t: arrival(row, t, diagonal, f_recv).wait_recv())
-                if place == 0:
-                    for k in range(n_rows):
-                        load_b(k).wait()
-                step = TILE
-                count = EARLY // step
-                split = (count * 3) // 4
-                multiply(row, 0, split, step)
+                for k in range(loaded, row + 1):
+                    load_b(k).wait()
+                loaded = max(loaded, row + 1)
+                split = EARLY // (2 * TILE) * TILE
+                multiply(row, 0, split)
                 if place + 1 < n_rows:
                     relay(sequence[place + 1])
-                multiply(row, split, count, step)
+                multiply(row, split, EARLY)
 
             for row, t in blocks:
                 def drain(row=row, t=t):

time: 71.9 us -> 61.4 us (0.85)
  Pallas kernels: 71.8 us -> 61.1 us
    pallas_call x1, Pallas kernels: 54.1 us -> 43.4 us  [local_product(): pl.pallas_call(gather_kernel, out_shape=tuple((pltpu.VMEM((BLOCK, EARLY),...]
where the time goes in v2:
time: 61.4 us; the launch traced here: 61.3 us
  Pallas kernels  61.1 us (100%)
    pallas_call x1, Pallas kernels, local_product(): pl.pallas_call(gather_kernel, out_shape=tuple((pltpu.VMEM((BLOCK, EARLY),...  43.4 us
    pallas_call x1, Pallas kernels, local_product(): pl.pallas_call(finish_kernel, out_shape=jax.ShapeDtypeStruct((order, widt...  17.7 us

profile of v2, /device:TPU:0, one launch (start us, length us, event | category | flops | bytes accessed | tf_op | source)
XLA Modules:
  0.0 61.3 jit_solution(13310132274456844494)
XLA Ops:
  0.0 43.4 %gather_and_multiply.1 = (bf16[256,5632]{1,0:T(8,128)(2,1)S(1)}, bf16[256,5632]{1,0:T(8,128)(2,1)S(1)}, bf16[256,5632]{1,0:T(8,128)(2,1)S(1)}, bf16[256,5632]{1,...) custom-call(bf16[2048,512]{1,0:T(8,128)(2,1)} %l_ref.1, ...), custom_call_target="tpu_custom_call" | custom-call | tf_op jit(solution)/shard_map/gather_and_multiply/pallas_call | solution.py:137
  43.4 17.7 %finish.1 = bf16[2048,8192]{1,0:T(8,128)(2,1)} custom-call(bf16[256,5632]{1,0:T(8,128)(2,1)S(1)} %get-tuple-element.21.refs_0_, bf16[256,5632]{1,0:T(8,128)(2,1)S(1)} %get-tuple-element.22.refs_1_, bf16[256,5632]{1,0:T(8,128)(2,1)S(1)} %get-tuple-element.23.refs_2_, bf16[256,5632]{1,0:T(8,128)(2,1)S(1)} %get-tuple-element.24.refs_3_, ...), custom_call_target="tpu_custom_call" | custom-call | tf_op jit(solution)/shard_map/finish/pallas_call | solution.py:186

commit v3 on v2

--- a/solution.py
+++ b/solution.py
@@ -41,7 +41,7 @@
 
         def gather_kernel(l_ref, b_ref, *refs):
             x_refs, l_refs = refs[:n_rows], refs[n_rows:2 * n_rows]
-            b_vmem, b_sem, own_sem, x_send, x_recv, p_send, p_recv, f_send, f_recv = refs[2 * n_rows:]
+            b_first, b_vmem, b_sem, own_sem, x_send, x_recv, p_send, p_recv, f_send, f_recv = refs[2 * n_rows:]
             me = lax.axis_index("col")
             across = lax.rem(me + 2, group)
             partner = me + 1 - 2 * lax.rem(me, 2)
@@ -83,6 +83,7 @@
                 rows = pl.ds(k * BLOCK, BLOCK)
                 return pltpu.make_async_copy(b_ref.at[rows, pl.ds(0, EARLY)], b_vmem.at[rows, :], b_sem.at[k])
 
+            first_late = pltpu.make_async_copy(b_ref.at[:, pl.ds(EARLY, TILE)], b_first, b_sem.at[n_rows])
             sequence = [3, 7, 6, 5, 4, 2, 1, 0]
             blocks = [(row, t) for row in sequence for t in range(per_dev)]
             for row, t in blocks:
@@ -94,6 +95,7 @@
                 when(held(row, me, t), start_near)
             for k in range(n_rows):
                 load_b(k).start()
+            first_late.start()
 
             def relay(row):
                 for t in range(per_dev):
@@ -124,6 +126,7 @@
                     relay(sequence[place + 1])
                 multiply(row, split, EARLY)
 
+            first_late.wait()
             for row, t in blocks:
                 def drain(row=row, t=t):
                     send(row, t, across, x_send, x_recv).wait_send()
@@ -137,61 +140,76 @@
         gathered = pl.pallas_call(
             gather_kernel,
             out_shape=tuple(pltpu.VMEM((BLOCK, EARLY), dtype) for _ in range(n_rows))
-            + tuple(pltpu.VMEM((BLOCK, BLOCK * (i + 1)), dtype) for i in range(n_rows)),
+            + tuple(pltpu.VMEM((BLOCK, BLOCK * (i + 1)), dtype) for i in range(n_rows))
+            + (pltpu.VMEM((order, TILE), dtype),),
             in_specs=[hbm, hbm],
-            out_specs=(vmem,) * (2 * n_rows),
-            scratch_shapes=[pltpu.VMEM((order, EARLY), dtype), dma((n_rows,))] + [dma((n_rows, per_dev))] * 7,
+            out_specs=(vmem,) * (2 * n_rows + 1),
+            scratch_shapes=[pltpu.VMEM((order, EARLY), dtype), dma((n_rows + 1,))] + [dma((n_rows, per_dev))] * 7,
             compiler_params=pltpu.CompilerParams(
-                collective_id=0, has_side_effects=True, vmem_limit_bytes=27 * MIB),
+                collective_id=0, has_side_effects=True, vmem_limit_bytes=24 * MIB),
             name="gather_and_multiply",
         )(l_cols, b_cols)
 
         def finish_kernel(*refs):
             x_refs, l_refs = refs[:n_rows], refs[n_rows:2 * n_rows]
-            b_ref, out_ref, b_vmem, x_vmem, b_sem, x_sem, early_sem = refs[2 * n_rows:]
+            b_first, b_ref, out_ref, b_vmem, x_vmem, b_sem, x_sem, early_sem = refs[2 * n_rows:]
 
             def load_b(n):
-                return pltpu.make_async_copy(
-                    b_ref.at[:, pl.ds(pl.multiple_of(EARLY + n * TILE, TILE), TILE)], b_vmem.at[n], b_sem.at[n])
+                cols = pl.ds(pl.multiple_of(EARLY + n * TILE, TILE), TILE)
+                return pltpu.make_async_copy(b_ref.at[:, cols], b_vmem.at[n - 1], b_sem.at[n - 1])
 
             def put_early(row):
                 return pltpu.make_async_copy(
                     x_refs[row], out_ref.at[pl.ds(row * BLOCK, BLOCK), pl.ds(0, EARLY)], early_sem.at[row])
 
-            def put_late(n):
-                return pltpu.make_async_copy(
-                    x_vmem.at[n], out_ref.at[:, pl.ds(pl.multiple_of(EARLY + n * TILE, TILE), TILE)], x_sem.at[n])
-
-            for n in range(n_late):
-                load_b(n).start()
-            for row in range(n_rows):
+            def put_late(n, row):
+                rows = pl.ds(row * BLOCK, BLOCK)
+                cols = pl.ds(pl.multiple_of(EARLY + n * TILE, TILE), TILE)
+                return pltpu.make_async_copy(x_vmem.at[n, rows, :], out_ref.at[rows, cols], x_sem.at[n, row])
+
+            def multiply(n, b_tile):
+                for row in range(n_rows - 1, -1, -1):
+                    x_vmem[n, pl.ds(row * BLOCK, BLOCK), :] = jnp.dot(
+                        l_refs[row][...], b_tile[pl.ds(0, (row + 1) * BLOCK), :],
+                        preferred_element_type=jnp.float32).astype(dtype)
+                    put_late(n, row).start()
+
+            load_b(1).start()
+            load_b(2).start()
+            for row in range(n_rows - 1, 4, -1):
                 put_early(row).start()
+            multiply(0, b_first)
 
             def body(n, carry):
+                @pl.when(n + 2 < n_late)
+                def _():
+                    load_b(n + 2).start()
+                for row in range(5):
+                    when(n == 1 + row // 2, lambda row=row: put_early(row).start())
                 load_b(n).wait()
-                for row in range(n_rows - 1, -1, -1):
-                    depth = (row + 1) * BLOCK
-                    x_vmem[n, pl.ds(row * BLOCK, BLOCK), :] = jnp.dot(
-                        l_refs[row][...], b_vmem[n, pl.ds(0, depth), :],
-                        preferred_element_type=jnp.float32).astype(dtype)
-                put_late(n).start()
+                multiply(n, b_vmem.at[n - 1])
                 return carry
 
-            lax.fori_loop(0, n_late, body, 0)
-            for n in range(n_late):
-                put_late(n).wait()
+            lax.fori_loop(1, n_late, body, 0)
             for row in range(n_rows):
                 put_early(row).wait()
+
+            def drain(n, carry):
+                for row in range(n_rows):
+                    put_late(n, row).wait()
+                return carry
+
+            lax.fori_loop(0, n_late, drain, 0)
 
         return pl.pallas_call(
             finish_kernel,
             out_shape=jax.ShapeDtypeStruct((order, width), dtype),
-            in_specs=[vmem] * (2 * n_rows) + [hbm],
+            in_specs=[vmem] * (2 * n_rows + 1) + [hbm],
             out_specs=hbm,
             scratch_shapes=[
-                pltpu.VMEM((n_late, order, TILE), dtype), pltpu.VMEM((n_late, order, TILE), dtype),
-                dma((n_late,)), dma((n_late,)), dma((n_rows,))],
-            compiler_params=pltpu.CompilerParams(vmem_limit_bytes=26 * MIB),
+                pltpu.VMEM((n_late - 1, order, TILE), dtype), pltpu.VMEM((n_late, order, TILE), dtype),
+                dma((n_late - 1,)), dma((n_late, n_rows)), dma((n_rows,))],
+            compiler_params=pltpu.CompilerParams(vmem_limit_bytes=20 * MIB),
             name="finish",
         )(*gathered, b_cols)
 

time: 61.4 us -> 60.6 us (0.987)
  Pallas kernels: 61.1 us -> 60.4 us
    pallas_call x1, Pallas kernels: 17.7 us -> 17 us  [local_product(): pl.pallas_call(finish_kernel, out_shape=jax.ShapeDtypeStruct((order, widt...]
where the time goes in v3:
time: 60.6 us
  Pallas kernels  60.4 us (100%)
    pallas_call x1, Pallas kernels, local_product(): pl.pallas_call(gather_kernel, out_shape=tuple((pltpu.VMEM((BLOCK, EARLY),...  43.4 us
    pallas_call x1, Pallas kernels, local_product(): pl.pallas_call(finish_kernel, out_shape=jax.ShapeDtypeStruct((order, widt...  17 us

profile of v3, /device:TPU:0, one launch (start us, length us, event | category | flops | bytes accessed | tf_op | source)
XLA Modules:
  0.0 60.6 jit_solution(15946678756590743872)
XLA Ops:
  0.0 43.4 %gather_and_multiply.1 = (bf16[256,5632]{1,0:T(8,128)(2,1)S(1)}, bf16[256,5632]{1,0:T(8,128)(2,1)S(1)}, bf16[256,5632]{1,0:T(8,128)(2,1)S(1)}, bf16[256,5632]{1,...) custom-call(bf16[2048,512]{1,0:T(8,128)(2,1)} %l_ref.1, ...), custom_call_target="tpu_custom_call" | custom-call | tf_op jit(solution)/shard_map/gather_and_multiply/pallas_call | solution.py:140
  43.4 17.0 %finish.1 = bf16[2048,8192]{1,0:T(8,128)(2,1)} custom-call(bf16[256,5632]{1,0:T(8,128)(2,1)S(1)} %get-tuple-element.22.refs_0_, bf16[256,5632]{1,0:T(8,128)(2,1)S(1)} %get-tuple-element.23.refs_1_, bf16[256,5632]{1,0:T(8,128)(2,1)S(1)} %get-tuple-element.24.refs_2_, bf16[256,5632]{1,0:T(8,128)(2,1)S(1)} %get-tuple-element.25.refs_3_, ...), custom_call_target="tpu_custom_call" | custom-call | tf_op jit(solution)/shard_map/finish/pallas_call | solution.py:204

commit v4 on v3

--- a/solution.py
+++ b/solution.py
@@ -39,9 +39,12 @@
                 return False
             return owner + low <= row
 
+        def late_place(k):
+            return pl.ds((n_rows - 1 - k // 2) * BLOCK, BLOCK), (k % 2) * late
+
         def gather_kernel(l_ref, b_ref, *refs):
             x_refs, l_refs = refs[:n_rows], refs[n_rows:2 * n_rows]
-            b_first, b_vmem, b_sem, own_sem, x_send, x_recv, p_send, p_recv, f_send, f_recv = refs[2 * n_rows:]
+            b_vmem, b_sem, late_sem, own_sem, x_send, x_recv, p_send, p_recv, f_send, f_recv = refs[2 * n_rows:]
             me = lax.axis_index("col")
             across = lax.rem(me + 2, group)
             partner = me + 1 - 2 * lax.rem(me, 2)
@@ -83,7 +86,11 @@
                 rows = pl.ds(k * BLOCK, BLOCK)
                 return pltpu.make_async_copy(b_ref.at[rows, pl.ds(0, EARLY)], b_vmem.at[rows, :], b_sem.at[k])
 
-            first_late = pltpu.make_async_copy(b_ref.at[:, pl.ds(EARLY, TILE)], b_first, b_sem.at[n_rows])
+            def load_late(k):
+                rows, start = late_place(k)
+                return pltpu.make_async_copy(
+                    b_ref.at[pl.ds(k * BLOCK, BLOCK), pl.ds(EARLY, late)], b_vmem.at[rows, pl.ds(start, late)], late_sem.at[k])
+
             sequence = [3, 7, 6, 5, 4, 2, 1, 0]
             blocks = [(row, t) for row in sequence for t in range(per_dev)]
             for row, t in blocks:
@@ -95,7 +102,6 @@
                 when(held(row, me, t), start_near)
             for k in range(n_rows):
                 load_b(k).start()
-            first_late.start()
 
             def relay(row):
                 for t in range(per_dev):
@@ -125,8 +131,12 @@
                 if place + 1 < n_rows:
                     relay(sequence[place + 1])
                 multiply(row, split, EARLY)
-
-            first_late.wait()
+                if row >= n_rows // 2:
+                    for k in range(2 * (n_rows - 1 - row), 2 * (n_rows - row)):
+                        load_late(k).start()
+
+            for k in range(n_rows):
+                load_late(k).wait()
             for row, t in blocks:
                 def drain(row=row, t=t):
                     send(row, t, across, x_send, x_recv).wait_send()
@@ -136,27 +146,23 @@
 
         dma = pltpu.SemaphoreType.DMA
         vmem = pl.BlockSpec(memory_space=pltpu.VMEM)
-        hbm = pl.BlockSpec(memory_space=pl.ANY)
+        hbm = pl.BlockSpec(memory_space=pltpu.HBM)
         gathered = pl.pallas_call(
             gather_kernel,
             out_shape=tuple(pltpu.VMEM((BLOCK, EARLY), dtype) for _ in range(n_rows))
             + tuple(pltpu.VMEM((BLOCK, BLOCK * (i + 1)), dtype) for i in range(n_rows))
-            + (pltpu.VMEM((order, TILE), dtype),),
+            + (pltpu.VMEM((order, EARLY), dtype),),
             in_specs=[hbm, hbm],
             out_specs=(vmem,) * (2 * n_rows + 1),
-            scratch_shapes=[pltpu.VMEM((order, EARLY), dtype), dma((n_rows + 1,))] + [dma((n_rows, per_dev))] * 7,
+            scratch_shapes=[dma((n_rows,)), dma((n_rows,))] + [dma((n_rows, per_dev))] * 7,
             compiler_params=pltpu.CompilerParams(
-                collective_id=0, has_side_effects=True, vmem_limit_bytes=24 * MIB),
+                collective_id=0, has_side_effects=True, vmem_limit_bytes=5 * MIB),
             name="gather_and_multiply",
         )(l_cols, b_cols)
 
         def finish_kernel(*refs):
             x_refs, l_refs = refs[:n_rows], refs[n_rows:2 * n_rows]
-            b_first, b_ref, out_ref, b_vmem, x_vmem, b_sem, x_sem, early_sem = refs[2 * n_rows:]
-
-            def load_b(n):
-                cols = pl.ds(pl.multiple_of(EARLY + n * TILE, TILE), TILE)
-                return pltpu.make_async_copy(b_ref.at[:, cols], b_vmem.at[n - 1], b_sem.at[n - 1])
+            b_vmem, out_ref, x_vmem, x_sem, early_sem = refs[2 * n_rows:]
 
             def put_early(row):
                 return pltpu.make_async_copy(
@@ -165,52 +171,48 @@
             def put_late(n, row):
                 rows = pl.ds(row * BLOCK, BLOCK)
                 cols = pl.ds(pl.multiple_of(EARLY + n * TILE, TILE), TILE)
-                return pltpu.make_async_copy(x_vmem.at[n, rows, :], out_ref.at[rows, cols], x_sem.at[n, row])
-
-            def multiply(n, b_tile):
-                for row in range(n_rows - 1, -1, -1):
-                    x_vmem[n, pl.ds(row * BLOCK, BLOCK), :] = jnp.dot(
-                        l_refs[row][...], b_tile[pl.ds(0, (row + 1) * BLOCK), :],
-                        preferred_element_type=jnp.float32).astype(dtype)
-                    put_late(n, row).start()
-
-            load_b(1).start()
-            load_b(2).start()
+                slot = lax.rem(n, 2)
+                return pltpu.make_async_copy(x_vmem.at[slot, rows, :], out_ref.at[rows, cols], x_sem.at[slot, row])
+
             for row in range(n_rows - 1, 4, -1):
                 put_early(row).start()
-            multiply(0, b_first)
 
             def body(n, carry):
-                @pl.when(n + 2 < n_late)
-                def _():
-                    load_b(n + 2).start()
                 for row in range(5):
                     when(n == 1 + row // 2, lambda row=row: put_early(row).start())
-                load_b(n).wait()
-                multiply(n, b_vmem.at[n - 1])
+
+                @pl.when(n >= 2)
+                def _():
+                    for row in range(n_rows):
+                        put_late(n - 2, row).wait()
+
+                for row in range(n_rows - 1, -1, -1):
+                    total = None
+                    for k in range(row + 1):
+                        rows, start = late_place(k)
+                        cols = pl.ds(pl.multiple_of(start + n * TILE, TILE), TILE)
+                        term = jnp.dot(l_refs[row][:, k * BLOCK:(k + 1) * BLOCK], b_vmem[rows, cols],
+                                       preferred_element_type=jnp.float32)
+                        total = term if total is None else total + term
+                    x_vmem[lax.rem(n, 2), pl.ds(row * BLOCK, BLOCK), :] = total.astype(dtype)
+                    put_late(n, row).start()
                 return carry
 
-            lax.fori_loop(1, n_late, body, 0)
+            lax.fori_loop(0, n_late, body, 0)
             for row in range(n_rows):
                 put_early(row).wait()
-
-            def drain(n, carry):
+            for n in range(n_late - 2, n_late):
                 for row in range(n_rows):
                     put_late(n, row).wait()
-                return carry
-
-            lax.fori_loop(0, n_late, drain, 0)
 
         return pl.pallas_call(
             finish_kernel,
             out_shape=jax.ShapeDtypeStruct((order, width), dtype),
-            in_specs=[vmem] * (2 * n_rows + 1) + [hbm],
+            in_specs=[vmem] * (2 * n_rows + 1),
             out_specs=hbm,
-            scratch_shapes=[
-                pltpu.VMEM((n_late - 1, order, TILE), dtype), pltpu.VMEM((n_late, order, TILE), dtype),
-                dma((n_late - 1,)), dma((n_late, n_rows)), dma((n_rows,))],
-            compiler_params=pltpu.CompilerParams(vmem_limit_bytes=20 * MIB),
+            scratch_shapes=[pltpu.VMEM((2, order, TILE), dtype), dma((2, n_rows)), dma((n_rows,))],
+            compiler_params=pltpu.CompilerParams(vmem_limit_bytes=5 * MIB),
             name="finish",
-        )(*gathered, b_cols)
+        )(*gathered)
 
     return jax.shard_map(local_product, mesh=mesh, in_specs=(P("batch", "col"), P("batch", "col")), out_specs=P("batch", "col"), check_vma=False)

time: 60.6 us -> 57.8 us (0.954)
  Pallas kernels: 60.4 us -> 57.6 us
    pallas_call x1, Pallas kernels: 17 us -> 14.1 us  [local_product(): pl.pallas_call(finish_kernel, out_shape=jax.ShapeDtypeStruct((order, widt...]
where the time goes in v4:
time: 57.8 us
  Pallas kernels  57.6 us (100%)
    pallas_call x1, Pallas kernels, local_product(): pl.pallas_call(gather_kernel, out_shape=tuple((pltpu.VMEM((BLOCK, EARLY),...  43.5 us
    pallas_call x1, Pallas kernels, local_product(): pl.pallas_call(finish_kernel, out_shape=jax.ShapeDtypeStruct((order, widt...  14.1 us

profile of v4, /device:TPU:0, one launch (start us, length us, event | category | flops | bytes accessed | tf_op | source)
XLA Modules:
  0.0 57.8 jit_solution(16392530238489910951)
XLA Ops:
  0.0 43.5 %gather_and_multiply.1 = (bf16[256,5632]{1,0:T(8,128)(2,1)S(1)}, bf16[256,5632]{1,0:T(8,128)(2,1)S(1)}, bf16[256,5632]{1,0:T(8,128)(2,1)S(1)}, bf16[256,5632]{1,...) custom-call(bf16[2048,512]{1,0:T(8,128)(2,1)} %l_ref.1, ...), custom_call_target="tpu_custom_call" | custom-call | tf_op jit(solution)/shard_map/gather_and_multiply/pallas_call | solution.py:150
  43.5 14.1 %finish.1 = bf16[2048,8192]{1,0:T(8,128)(2,1)} custom-call(bf16[256,5632]{1,0:T(8,128)(2,1)S(1)} %get-tuple-element.22.refs_0_, bf16[256,5632]{1,0:T(8,128)(2,1)S(1)} %get-tuple-element.23.refs_1_, bf16[256,5632]{1,0:T(8,128)(2,1)S(1)} %get-tuple-element.24.refs_2_, bf16[256,5632]{1,0:T(8,128)(2,1)S(1)} %get-tuple-element.25.refs_3_, ...), custom_call_target="tpu_custom_call" | custom-call | tf_op jit(solution)/shard_map/finish/pallas_call | solution.py:208

commit v5 on v4

--- a/solution.py
+++ b/solution.py
@@ -44,7 +44,7 @@
 
         def gather_kernel(l_ref, b_ref, *refs):
             x_refs, l_refs = refs[:n_rows], refs[n_rows:2 * n_rows]
-            b_vmem, b_sem, late_sem, own_sem, x_send, x_recv, p_send, p_recv, f_send, f_recv = refs[2 * n_rows:]
+            b_vmem, partial, b_sem, late_sem, own_sem, x_send, x_recv, p_send, p_recv, f_send, f_recv = refs[2 * n_rows:]
             me = lax.axis_index("col")
             across = lax.rem(me + 2, group)
             partner = me + 1 - 2 * lax.rem(me, 2)
@@ -82,8 +82,11 @@
                     src_ref=block, dst_ref=block, send_sem=f_send.at[row, t], recv_sem=f_recv.at[row, t],
                     device_id={"col": partner}, device_id_type=MESH)
 
+            near = me - lax.rem(me, 2)
+            far = 2 - near
+
             def load_b(k):
-                rows = pl.ds(k * BLOCK, BLOCK)
+                rows = pl.ds(pl.multiple_of(k * BLOCK, BLOCK), BLOCK)
                 return pltpu.make_async_copy(b_ref.at[rows, pl.ds(0, EARLY)], b_vmem.at[rows, :], b_sem.at[k])
 
             def load_late(k):
@@ -91,17 +94,20 @@
                 return pltpu.make_async_copy(
                     b_ref.at[pl.ds(k * BLOCK, BLOCK), pl.ds(EARLY, late)], b_vmem.at[rows, pl.ds(start, late)], late_sem.at[k])
 
-            sequence = [3, 7, 6, 5, 4, 2, 1, 0]
+            sequence = [3, 4, 5, 6, 7, 2, 1, 0]
+            last = n_rows - 1
             blocks = [(row, t) for row in sequence for t in range(per_dev)]
             for row, t in blocks:
                 when(held(row, me, t), lambda row=row, t=t: send(row, t, across, x_send, x_recv).start())
-            for row, t in blocks:
+            for row, t in [(last, t) for t in range(per_dev)] + [b for b in blocks if b[0] != last]:
                 def start_near(row=row, t=t):
                     send(row, t, partner, p_send, p_recv).start()
                     own_copy(row, t).start()
                 when(held(row, me, t), start_near)
-            for k in range(n_rows):
-                load_b(k).start()
+            for side in (near, far):
+                for t in range(per_dev):
+                    for c in range(2):
+                        load_b(side + group * t + c).start()
 
             def relay(row):
                 for t in range(per_dev):
@@ -110,30 +116,59 @@
                         forward(row, t).start()
                     when(held(row, across, t), step)
 
-            def multiply(row, start, stop):
-                depth = (row + 1) * BLOCK
-                x_refs[row][:, start:stop] = jnp.dot(
-                    l_refs[row][...], b_vmem[:depth, start:stop],
-                    preferred_element_type=jnp.float32).astype(dtype)
-
-            relay(sequence[0])
-            loaded = 0
-            for place, row in enumerate(sequence):
+            def wait_near(row):
                 for t in range(per_dev):
                     when(held(row, me, t), lambda t=t: own_copy(row, t).wait())
                     when(held(row, partner, t), lambda t=t: arrival(row, t, partner, p_recv).wait_recv())
+
+            def half_product(side, start, stop):
+                total = None
+                for t in range(per_dev):
+                    depth = pl.ds(pl.multiple_of((side + group * t) * BLOCK, 2 * BLOCK), 2 * BLOCK)
+                    term = jnp.dot(l_refs[last][:, depth], b_vmem[depth, start:stop], preferred_element_type=jnp.float32)
+                    total = term if total is None else total + term
+                return total
+
+            def multiply(row, start, stop):
+                if row == last:
+                    for n in range(start, stop, TILE):
+                        total = partial[:, n:n + TILE] + half_product(far, n, n + TILE)
+                        x_refs[row][:, n:n + TILE] = total.astype(dtype)
+                    return
+                x_refs[row][:, start:stop] = jnp.dot(
+                    l_refs[row][...], b_vmem[:(row + 1) * BLOCK, start:stop],
+                    preferred_element_type=jnp.float32).astype(dtype)
+
+            wait_near(last)
+            for t in range(per_dev):
+                for c in range(2):
+                    load_b(near + group * t + c).wait()
+            middle = EARLY // (2 * TILE) * TILE
+            for start in range(0, EARLY, TILE):
+                if start == middle:
+                    relay(sequence[0])
+                partial[:, start:start + TILE] = half_product(near, start, start + TILE)
+            for t in range(per_dev):
+                for c in range(2):
+                    load_b(far + group * t + c).wait()
+
+            freed = []
+            for place, row in enumerate(sequence):
+                if row != last:
+                    wait_near(row)
+                for t in range(per_dev):
                     when(held(row, diagonal, t), lambda t=t: arrival(row, t, diagonal, f_recv).wait_recv())
-                for k in range(loaded, row + 1):
-                    load_b(k).wait()
-                loaded = max(loaded, row + 1)
-                split = EARLY // (2 * TILE) * TILE
+                split = EARLY // TILE * 3 // 4 * TILE
                 multiply(row, 0, split)
                 if place + 1 < n_rows:
                     relay(sequence[place + 1])
                 multiply(row, split, EARLY)
-                if row >= n_rows // 2:
-                    for k in range(2 * (n_rows - 1 - row), 2 * (n_rows - row)):
-                        load_late(k).start()
+                free = [k for k in range(n_rows // 2, n_rows) if all(k > r for r in sequence[place + 1:])]
+                for k in free:
+                    if k not in freed:
+                        freed.append(k)
+                        for piece in range(2 * (last - k), 2 * (n_rows - k)):
+                            load_late(piece).start()
 
             for k in range(n_rows):
                 load_late(k).wait()
@@ -154,9 +189,9 @@
             + (pltpu.VMEM((order, EARLY), dtype),),
             in_specs=[hbm, hbm],
             out_specs=(vmem,) * (2 * n_rows + 1),
-            scratch_shapes=[dma((n_rows,)), dma((n_rows,))] + [dma((n_rows, per_dev))] * 7,
+            scratch_shapes=[pltpu.VMEM((BLOCK, EARLY), jnp.float32), dma((n_rows,)), dma((n_rows,))] + [dma((n_rows, per_dev))] * 7,
             compiler_params=pltpu.CompilerParams(
-                collective_id=0, has_side_effects=True, vmem_limit_bytes=5 * MIB),
+                collective_id=0, has_side_effects=True, vmem_limit_bytes=8 * MIB),
             name="gather_and_multiply",
         )(l_cols, b_cols)
 

time: 57.8 us -> 56 us (0.969)
  the two profiles are of different devices: /device:TPU:0 before, /device:TPU:3 now
where the time goes in v5:
time: 56 us; the launch traced here: 55.9 us
  Pallas kernels  55.7 us (99%)
    pallas_call x1, Pallas kernels, local_product(): pl.pallas_call(gather_kernel, out_shape=tuple((pltpu.VMEM((BLOCK, EARLY),...  41.6 us
    pallas_call x1, Pallas kernels, local_product(): pl.pallas_call(finish_kernel, out_shape=jax.ShapeDtypeStruct((order, widt...  14.1 us

profile of v5, /device:TPU:3, one launch (start us, length us, event | category | flops | bytes accessed | tf_op | source)
XLA Modules:
  0.0 55.9 jit_solution(12717733951845593447)
XLA Ops:
  0.0 41.6 %gather_and_multiply.1 = (bf16[256,5632]{1,0:T(8,128)(2,1)S(1)}, bf16[256,5632]{1,0:T(8,128)(2,1)S(1)}, bf16[256,5632]{1,0:T(8,128)(2,1)S(1)}, bf16[256,5632]{1,...) custom-call(bf16[2048,512]{1,0:T(8,128)(2,1)} %l_ref.1, ...), custom_call_target="tpu_custom_call" | custom-call | tf_op jit(solution)/shard_map/gather_and_multiply/pallas_call | solution.py:185
  41.6 14.1 %finish.1 = bf16[2048,8192]{1,0:T(8,128)(2,1)} custom-call(bf16[256,5632]{1,0:T(8,128)(2,1)S(1)} %get-tuple-element.22.refs_0_, bf16[256,5632]{1,0:T(8,128)(2,1)S(1)} %get-tuple-element.23.refs_1_, bf16[256,5632]{1,0:T(8,128)(2,1)S(1)} %get-tuple-element.24.refs_2_, bf16[256,5632]{1,0:T(8,128)(2,1)S(1)} %get-tuple-element.25.refs_3_, ...), custom_call_target="tpu_custom_call" | custom-call | tf_op jit(solution)/shard_map/finish/pallas_call | solution.py:243

commit v6 on v5

--- a/solution.py
+++ b/solution.py
@@ -50,11 +50,6 @@
             partner = me + 1 - 2 * lax.rem(me, 2)
             diagonal = lax.rem(partner + 2, group)
 
-            barrier = pltpu.get_barrier_semaphore()
-            for peer in (partner, across):
-                pl.semaphore_signal(barrier, inc=1, device_id={"col": peer}, device_id_type=MESH)
-            pl.semaphore_wait(barrier, 2)
-
             def panel(row, owner, t):
                 start = pl.multiple_of((owner + group * t) * BLOCK, BLOCK)
                 return l_refs[row].at[:, pl.ds(start, BLOCK)]
@@ -67,7 +62,7 @@
 
             def send(row, t, peer, send_sem, recv_sem):
                 return pltpu.make_async_remote_copy(
-                    src_ref=mine(row, t), dst_ref=panel(row, me, t), send_sem=send_sem.at[row, t],
+                    src_ref=panel(row, me, t), dst_ref=panel(row, me, t), send_sem=send_sem.at[row, t],
                     recv_sem=recv_sem.at[row, t], device_id={"col": peer}, device_id_type=MESH)
 
             def arrival(row, t, owner, recv_sem):
@@ -97,17 +92,25 @@
             sequence = [3, 4, 5, 6, 7, 2, 1, 0]
             last = n_rows - 1
             blocks = [(row, t) for row in sequence for t in range(per_dev)]
+            barrier = pltpu.get_barrier_semaphore()
+            for peer in (partner, across):
+                pl.semaphore_signal(barrier, inc=1, device_id={"col": peer}, device_id_type=MESH)
             for row, t in blocks:
-                when(held(row, me, t), lambda row=row, t=t: send(row, t, across, x_send, x_recv).start())
-            for row, t in [(last, t) for t in range(per_dev)] + [b for b in blocks if b[0] != last]:
-                def start_near(row=row, t=t):
-                    send(row, t, partner, p_send, p_recv).start()
-                    own_copy(row, t).start()
-                when(held(row, me, t), start_near)
+                when(held(row, me, t), lambda row=row, t=t: own_copy(row, t).start())
             for side in (near, far):
                 for t in range(per_dev):
                     for c in range(2):
                         load_b(side + group * t + c).start()
+
+            pl.semaphore_wait(barrier, 2)
+
+            for row, t in blocks:
+                def start_across(row=row, t=t):
+                    own_copy(row, t).wait()
+                    send(row, t, across, x_send, x_recv).start()
+                when(held(row, me, t), start_across)
+            for row, t in [(last, t) for t in range(per_dev)] + [b for b in blocks if b[0] != last]:
+                when(held(row, me, t), lambda row=row, t=t: send(row, t, partner, p_send, p_recv).start())
 
             def relay(row):
                 for t in range(per_dev):
@@ -118,7 +121,6 @@
 
             def wait_near(row):
                 for t in range(per_dev):
-                    when(held(row, me, t), lambda t=t: own_copy(row, t).wait())
                     when(held(row, partner, t), lambda t=t: arrival(row, t, partner, p_recv).wait_recv())
 
             def half_product(side, start, stop):

time: 56 us -> 56 us (level)
  no operation moved by 1% of the time
where the time goes in v6:
time: 56 us; the launch traced here: 55.9 us
  Pallas kernels  55.7 us (99%)
    pallas_call x1, Pallas kernels, local_product(): pl.pallas_call(gather_kernel, out_shape=tuple((pltpu.VMEM((BLOCK, EARLY),...  41.6 us
    pallas_call x1, Pallas kernels, local_product(): pl.pallas_call(finish_kernel, out_shape=jax.ShapeDtypeStruct((order, widt...  14.1 us

profile of v6, /device:TPU:3, one launch (start us, length us, event | category | flops | bytes accessed | tf_op | source)
XLA Modules:
  0.0 55.9 jit_solution(11563426873569339861)
XLA Ops:
  0.0 41.6 %gather_and_multiply.1 = (bf16[256,5632]{1,0:T(8,128)(2,1)S(1)}, bf16[256,5632]{1,0:T(8,128)(2,1)S(1)}, bf16[256,5632]{1,0:T(8,128)(2,1)S(1)}, bf16[256,5632]{1,...) custom-call(bf16[2048,512]{1,0:T(8,128)(2,1)} %l_ref.1, ...), custom_call_target="tpu_custom_call" | custom-call | tf_op jit(solution)/shard_map/gather_and_multiply/pallas_call | solution.py:187
  41.7 14.1 %finish.1 = bf16[2048,8192]{1,0:T(8,128)(2,1)} custom-call(bf16[256,5632]{1,0:T(8,128)(2,1)S(1)} %get-tuple-element.22.refs_0_, bf16[256,5632]{1,0:T(8,128)(2,1)S(1)} %get-tuple-element.23.refs_1_, bf16[256,5632]{1,0:T(8,128)(2,1)S(1)} %get-tuple-element.24.refs_2_, bf16[256,5632]{1,0:T(8,128)(2,1)S(1)} %get-tuple-element.25.refs_3_, ...), custom_call_target="tpu_custom_call" | custom-call | tf_op jit(solution)/shard_map/finish/pallas_call | solution.py:245

commit v7 on v6

--- a/solution.py
+++ b/solution.py
@@ -39,12 +39,25 @@
                 return False
             return owner + low <= row
 
+        def pieces(row, t, owner):
+            full = [(0, BLOCK, BLOCK)]
+            high = row - group * t
+            if high >= group:
+                return [(True, full)]
+            if high < 0:
+                return []
+            half = BLOCK // 2
+            cases = [(owner == high, [(0, half, half), (half, half, BLOCK)])]
+            if high > 0:
+                cases.append((owner < high, full))
+            return cases
+
         def late_place(k):
             return pl.ds((n_rows - 1 - k // 2) * BLOCK, BLOCK), (k % 2) * late
 
         def gather_kernel(l_ref, b_ref, *refs):
             x_refs, l_refs = refs[:n_rows], refs[n_rows:2 * n_rows]
-            b_vmem, partial, b_sem, late_sem, own_sem, x_send, x_recv, p_send, p_recv, f_send, f_recv = refs[2 * n_rows:]
+            b_vmem, partial, b_sem, late_sem, own_sem, p_send, p_recv, x_send, x_recv, f_send, f_recv = refs[2 * n_rows:]
             me = lax.axis_index("col")
             across = lax.rem(me + 2, group)
             partner = me + 1 - 2 * lax.rem(me, 2)
@@ -60,22 +73,32 @@
             def own_copy(row, t):
                 return pltpu.make_async_copy(mine(row, t), panel(row, me, t), own_sem.at[row, t])
 
-            def send(row, t, peer, send_sem, recv_sem):
+            def remote(src, dst, send_sem, recv_sem, peer):
                 return pltpu.make_async_remote_copy(
-                    src_ref=panel(row, me, t), dst_ref=panel(row, me, t), send_sem=send_sem.at[row, t],
-                    recv_sem=recv_sem.at[row, t], device_id={"col": peer}, device_id_type=MESH)
-
-            def arrival(row, t, owner, recv_sem):
-                dst = panel(row, owner, t)
-                return pltpu.make_async_remote_copy(
-                    src_ref=dst, dst_ref=dst, send_sem=x_send.at[row, t], recv_sem=recv_sem.at[row, t],
-                    device_id={"col": partner}, device_id_type=MESH)
-
-            def forward(row, t):
-                block = panel(row, across, t)
-                return pltpu.make_async_remote_copy(
-                    src_ref=block, dst_ref=block, send_sem=f_send.at[row, t], recv_sem=f_recv.at[row, t],
-                    device_id={"col": partner}, device_id_type=MESH)
+                    src_ref=src, dst_ref=dst, send_sem=send_sem, recv_sem=recv_sem, device_id={"col": peer}, device_id_type=MESH)
+
+            def share(row, t, owner):
+                block = panel(row, owner, t)
+                return remote(block, block, p_send.at[row, t], p_recv.at[row, t], partner)
+
+            def parts(row, t, owner, send_sem, recv_sem, peer, act):
+                for cond, rects in pieces(row, t, owner):
+                    def run(rects=rects):
+                        for j, (first, rows, width) in enumerate(rects):
+                            start = pl.multiple_of((owner + group * t) * BLOCK, BLOCK)
+                            part = l_refs[row].at[pl.ds(first, rows), pl.ds(start, width)]
+                            act(j, remote(part, part, send_sem.at[row, t, j], recv_sem.at[row, t, j], peer))
+                    when(cond, run)
+
+            def parts_both(row, t, owner, act):
+                for cond, rects in pieces(row, t, owner):
+                    def run(rects=rects):
+                        for j, (first, rows, width) in enumerate(rects):
+                            start = pl.multiple_of((owner + group * t) * BLOCK, BLOCK)
+                            part = l_refs[row].at[pl.ds(first, rows), pl.ds(start, width)]
+                            act(remote(part, part, x_send.at[row, t, j], x_recv.at[row, t, j], across),
+                                remote(part, part, f_send.at[row, t, j], f_recv.at[row, t, j], partner))
+                    when(cond, run)
 
             near = me - lax.rem(me, 2)
             far = 2 - near
@@ -89,39 +112,44 @@
                 return pltpu.make_async_copy(
                     b_ref.at[pl.ds(k * BLOCK, BLOCK), pl.ds(EARLY, late)], b_vmem.at[rows, pl.ds(start, late)], late_sem.at[k])
 
-            sequence = [3, 4, 5, 6, 7, 2, 1, 0]
+            sequence = [3, 6, 5, 4, 7, 2, 1, 0]
+            before = [8, 8, 8, 8, 5, 5, 0, 0]
             last = n_rows - 1
             blocks = [(row, t) for row in sequence for t in range(per_dev)]
+            shared = [(last, t) for t in range(per_dev)] + [b for b in blocks if b[0] != last]
+
             barrier = pltpu.get_barrier_semaphore()
             for peer in (partner, across):
                 pl.semaphore_signal(barrier, inc=1, device_id={"col": peer}, device_id_type=MESH)
-            for row, t in blocks:
+            for row, t in shared:
                 when(held(row, me, t), lambda row=row, t=t: own_copy(row, t).start())
+            for row in range(n_rows):
+                def clear(row=row):
+                    l_refs[row][:BLOCK // 2, row * BLOCK + BLOCK // 2:] = jnp.zeros((BLOCK // 2, BLOCK // 2), dtype)
+                when(far == row % group // 2 * 2, clear)
+            for row, t in shared:
+                when(held(row, me, t), lambda row=row, t=t: own_copy(row, t).wait())
             for side in (near, far):
                 for t in range(per_dev):
                     for c in range(2):
                         load_b(side + group * t + c).start()
-
             pl.semaphore_wait(barrier, 2)
 
             for row, t in blocks:
-                def start_across(row=row, t=t):
-                    own_copy(row, t).wait()
-                    send(row, t, across, x_send, x_recv).start()
-                when(held(row, me, t), start_across)
-            for row, t in [(last, t) for t in range(per_dev)] + [b for b in blocks if b[0] != last]:
-                when(held(row, me, t), lambda row=row, t=t: send(row, t, partner, p_send, p_recv).start())
+                parts(row, t, me, x_send, x_recv, across, lambda j, copy: copy.start())
+            for row, t in shared:
+                when(held(row, me, t), lambda row=row, t=t: share(row, t, me).start())
 
             def relay(row):
-                for t in range(per_dev):
-                    def step(t=t):
-                        arrival(row, t, across, x_recv).wait_recv()
-                        forward(row, t).start()
-                    when(held(row, across, t), step)
+                def step(came, on):
+                    came.wait_recv()
+                    on.start()
+                for t in range(per_dev):
+                    parts_both(row, t, across, step)
 
             def wait_near(row):
                 for t in range(per_dev):
-                    when(held(row, partner, t), lambda t=t: arrival(row, t, partner, p_recv).wait_recv())
+                    when(held(row, partner, t), lambda t=t: share(row, t, partner).wait_recv())
 
             def half_product(side, start, stop):
                 total = None
@@ -159,9 +187,10 @@
                 if row != last:
                     wait_near(row)
                 for t in range(per_dev):
-                    when(held(row, diagonal, t), lambda t=t: arrival(row, t, diagonal, f_recv).wait_recv())
-                split = EARLY // TILE * 3 // 4 * TILE
-                multiply(row, 0, split)
+                    parts(row, t, diagonal, f_send, f_recv, partner, lambda j, copy: copy.wait_recv())
+                split = before[place] * TILE
+                if split:
+                    multiply(row, 0, split)
                 if place + 1 < n_rows:
                     relay(sequence[place + 1])
                 multiply(row, split, EARLY)
@@ -175,11 +204,9 @@
             for k in range(n_rows):
                 load_late(k).wait()
             for row, t in blocks:
-                def drain(row=row, t=t):
-                    send(row, t, across, x_send, x_recv).wait_send()
-                    send(row, t, partner, p_send, p_recv).wait_send()
-                when(held(row, me, t), drain)
-                when(held(row, across, t), lambda row=row, t=t: forward(row, t).wait_send())
+                parts(row, t, me, x_send, x_recv, across, lambda j, copy: copy.wait_send())
+                when(held(row, me, t), lambda row=row, t=t: share(row, t, me).wait_send())
+                parts(row, t, across, f_send, f_recv, partner, lambda j, copy: copy.wait_send())
 
         dma = pltpu.SemaphoreType.DMA
         vmem = pl.BlockSpec(memory_space=pltpu.VMEM)
@@ -191,7 +218,8 @@
             + (pltpu.VMEM((order, EARLY), dtype),),
             in_specs=[hbm, hbm],
             out_specs=(vmem,) * (2 * n_rows + 1),
-            scratch_shapes=[pltpu.VMEM((BLOCK, EARLY), jnp.float32), dma((n_rows,)), dma((n_rows,))] + [dma((n_rows, per_dev))] * 7,
+            scratch_shapes=[pltpu.VMEM((BLOCK, EARLY), jnp.float32), dma((n_rows,)), dma((n_rows,))]
+            + [dma((n_rows, per_dev))] * 3 + [dma((n_rows, per_dev, 2))] * 4,
             compiler_params=pltpu.CompilerParams(
                 collective_id=0, has_side_effects=True, vmem_limit_bytes=8 * MIB),
             name="gather_and_multiply",
@@ -207,35 +235,31 @@
 
             def put_late(n, row):
                 rows = pl.ds(row * BLOCK, BLOCK)
-                cols = pl.ds(pl.multiple_of(EARLY + n * TILE, TILE), TILE)
-                slot = lax.rem(n, 2)
+                cols = pl.ds(EARLY + n * TILE, TILE)
+                slot = n % 2
                 return pltpu.make_async_copy(x_vmem.at[slot, rows, :], out_ref.at[rows, cols], x_sem.at[slot, row])
 
             for row in range(n_rows - 1, 4, -1):
                 put_early(row).start()
 
-            def body(n, carry):
+            for n in range(n_late):
                 for row in range(5):
-                    when(n == 1 + row // 2, lambda row=row: put_early(row).start())
-
-                @pl.when(n >= 2)
-                def _():
+                    if n == 1 + row // 2:
+                        put_early(row).start()
+                if n >= 2:
                     for row in range(n_rows):
                         put_late(n - 2, row).wait()
-
                 for row in range(n_rows - 1, -1, -1):
                     total = None
                     for k in range(row + 1):
                         rows, start = late_place(k)
-                        cols = pl.ds(pl.multiple_of(start + n * TILE, TILE), TILE)
-                        term = jnp.dot(l_refs[row][:, k * BLOCK:(k + 1) * BLOCK], b_vmem[rows, cols],
+                        term = jnp.dot(l_refs[row][:, k * BLOCK:(k + 1) * BLOCK],
+                                       b_vmem[rows, start + n * TILE:start + (n + 1) * TILE],
                                        preferred_element_type=jnp.float32)
                         total = term if total is None else total + term
-                    x_vmem[lax.rem(n, 2), pl.ds(row * BLOCK, BLOCK), :] = total.astype(dtype)
+                    x_vmem[n % 2, row * BLOCK:(row + 1) * BLOCK, :] = total.astype(dtype)
                     put_late(n, row).start()
-                return carry
-
-            lax.fori_loop(0, n_late, body, 0)
+
             for row in range(n_rows):
                 put_early(row).wait()
             for n in range(n_late - 2, n_late):

time: 56 us -> 54.4 us (0.971)
  the two profiles are of different devices: /device:TPU:3 before, /device:TPU:0 now
where the time goes in v7:
time: 54.4 us; the launch traced here: 54.2 us
  Pallas kernels  54 us (99%)
    pallas_call x1, Pallas kernels, local_product(): pl.pallas_call(gather_kernel, out_shape=tuple((pltpu.VMEM((BLOCK, EARLY),...  39.9 us
    pallas_call x1, Pallas kernels, local_product(): pl.pallas_call(finish_kernel, out_shape=jax.ShapeDtypeStruct((order, widt...  14.1 us

profile of v7, /device:TPU:0, one launch (start us, length us, event | category | flops | bytes accessed | tf_op | source)
XLA Modules:
  0.0 54.2 jit_solution(15866731333125882449)
XLA Ops:
  0.0 39.9 %gather_and_multiply.1 = (bf16[256,5632]{1,0:T(8,128)(2,1)S(1)}, bf16[256,5632]{1,0:T(8,128)(2,1)S(1)}, bf16[256,5632]{1,0:T(8,128)(2,1)S(1)}, bf16[256,5632]{1,...) custom-call(bf16[2048,512]{1,0:T(8,128)(2,1)} %l_ref.1, ...), custom_call_target="tpu_custom_call" | custom-call | tf_op jit(solution)/shard_map/gather_and_multiply/pallas_call | solution.py:214
  39.9 14.1 %finish.1 = bf16[2048,8192]{1,0:T(8,128)(2,1)} custom-call(bf16[256,5632]{1,0:T(8,128)(2,1)S(1)} %get-tuple-element.22.refs_0_, bf16[256,5632]{1,0:T(8,128)(2,1)S(1)} %get-tuple-element.23.refs_1_, bf16[256,5632]{1,0:T(8,128)(2,1)S(1)} %get-tuple-element.24.refs_2_, bf16[256,5632]{1,0:T(8,128)(2,1)S(1)} %get-tuple-element.25.refs_3_, ...), custom_call_target="tpu_custom_call" | custom-call | tf_op jit(solution)/shard_map/finish/pallas_call | solution.py:269

commit v8 on v7

--- a/solution.py
+++ b/solution.py
@@ -52,8 +52,14 @@
                 cases.append((owner < high, full))
             return cases
 
+        def chip_sides():
+            me = lax.axis_index("col")
+            near = me - lax.rem(me, 2)
+            return near, 2 - near
+
         def late_place(k):
-            return pl.ds((n_rows - 1 - k // 2) * BLOCK, BLOCK), (k % 2) * late
+            block = chip_sides()[k // group] + group + k % group // 2
+            return pl.ds(pl.multiple_of(block * BLOCK, BLOCK), BLOCK), k % 2 * late
 
         def gather_kernel(l_ref, b_ref, *refs):
             x_refs, l_refs = refs[:n_rows], refs[n_rows:2 * n_rows]
@@ -100,8 +106,7 @@
                                 remote(part, part, f_send.at[row, t, j], f_recv.at[row, t, j], partner))
                     when(cond, run)
 
-            near = me - lax.rem(me, 2)
-            far = 2 - near
+            near, far = chip_sides()
 
             def load_b(k):
                 rows = pl.ds(pl.multiple_of(k * BLOCK, BLOCK), BLOCK)
@@ -182,7 +187,6 @@
                 for c in range(2):
                     load_b(far + group * t + c).wait()
 
-            freed = []
             for place, row in enumerate(sequence):
                 if row != last:
                     wait_near(row)
@@ -194,12 +198,12 @@
                 if place + 1 < n_rows:
                     relay(sequence[place + 1])
                 multiply(row, split, EARLY)
-                free = [k for k in range(n_rows // 2, n_rows) if all(k > r for r in sequence[place + 1:])]
-                for k in free:
-                    if k not in freed:
-                        freed.append(k)
-                        for piece in range(2 * (last - k), 2 * (n_rows - k)):
-                            load_late(piece).start()
+                if row == 4:
+                    for k in range(group):
+                        load_late(k).start()
+                if row == last:
+                    for k in range(group, n_rows):
+                        load_late(k).start()
 
             for k in range(n_rows):
                 load_late(k).wait()
@@ -227,53 +231,54 @@
 
         def finish_kernel(*refs):
             x_refs, l_refs = refs[:n_rows], refs[n_rows:2 * n_rows]
-            b_vmem, out_ref, x_vmem, x_sem, early_sem = refs[2 * n_rows:]
+            b_vmem, out_ref, x_late, late_sem, early_sem = refs[2 * n_rows:]
 
             def put_early(row):
                 return pltpu.make_async_copy(
                     x_refs[row], out_ref.at[pl.ds(row * BLOCK, BLOCK), pl.ds(0, EARLY)], early_sem.at[row])
 
-            def put_late(n, row):
-                rows = pl.ds(row * BLOCK, BLOCK)
-                cols = pl.ds(EARLY + n * TILE, TILE)
-                slot = n % 2
-                return pltpu.make_async_copy(x_vmem.at[slot, rows, :], out_ref.at[rows, cols], x_sem.at[slot, row])
-
-            for row in range(n_rows - 1, 4, -1):
+            def place(row):
+                return pl.ds(row // 2 * BLOCK, BLOCK), row % 2 * late
+
+            def tile(start, n):
+                return pl.ds(pl.multiple_of(start + n * TILE, TILE), TILE)
+
+            def put_late(row, n):
+                rows, start = place(row)
+                return pltpu.make_async_copy(
+                    x_late.at[rows, tile(start, n)], out_ref.at[pl.ds(row * BLOCK, BLOCK), tile(EARLY, n)], late_sem.at[n, row])
+
+            for row in range(n_rows - 1, -1, -1):
                 put_early(row).start()
-
-            for n in range(n_late):
-                for row in range(5):
-                    if n == 1 + row // 2:
-                        put_early(row).start()
-                if n >= 2:
-                    for row in range(n_rows):
-                        put_late(n - 2, row).wait()
+            def body(n, carry):
                 for row in range(n_rows - 1, -1, -1):
                     total = None
                     for k in range(row + 1):
                         rows, start = late_place(k)
-                        term = jnp.dot(l_refs[row][:, k * BLOCK:(k + 1) * BLOCK],
-                                       b_vmem[rows, start + n * TILE:start + (n + 1) * TILE],
+                        term = jnp.dot(l_refs[row][:, k * BLOCK:(k + 1) * BLOCK], b_vmem[rows, tile(start, n)],
                                        preferred_element_type=jnp.float32)
                         total = term if total is None else total + term
-                    x_vmem[n % 2, row * BLOCK:(row + 1) * BLOCK, :] = total.astype(dtype)
-                    put_late(n, row).start()
-
-            for row in range(n_rows):
+                    rows, start = place(row)
+                    x_late[rows, tile(start, n)] = total.astype(dtype)
+                for row in range(n_rows - 1, -1, -1):
+                    put_late(row, n).start()
+                return carry
+
+            lax.fori_loop(0, n_late, body, 0)
+            for row in range(n_rows - 1, -1, -1):
                 put_early(row).wait()
-            for n in range(n_late - 2, n_late):
-                for row in range(n_rows):
-                    put_late(n, row).wait()
+                for n in range(n_late):
+                    put_late(row, n).wait()
 
         return pl.pallas_call(
             finish_kernel,
-            out_shape=jax.ShapeDtypeStruct((order, width), dtype),
+            out_shape=(jax.ShapeDtypeStruct((order, width), dtype), pltpu.VMEM((order, EARLY), dtype)),
             in_specs=[vmem] * (2 * n_rows + 1),
-            out_specs=hbm,
-            scratch_shapes=[pltpu.VMEM((2, order, TILE), dtype), dma((2, n_rows)), dma((n_rows,))],
+            out_specs=(hbm, vmem),
+            input_output_aliases={2 * n_rows: 1},
+            scratch_shapes=[dma((n_late, n_rows)), dma((n_rows,))],
             compiler_params=pltpu.CompilerParams(vmem_limit_bytes=5 * MIB),
             name="finish",
-        )(*gathered)
+        )(*gathered)[0]
 
     return jax.shard_map(local_product, mesh=mesh, in_specs=(P("batch", "col"), P("batch", "col")), out_specs=P("batch", "col"), check_vma=False)

time: 54.4 us -> 60.9 us (1.12)
  Pallas kernels: 54 us -> 60.5 us
    pallas_call x1, Pallas kernels: 14.1 us -> 20.6 us  [local_product(): pl.pallas_call(finish_kernel, out_shape=(jax.ShapeDtypeStruct((order, wid...]
where the time goes in v8:
time: 60.9 us; the launch traced here: 60.7 us
  Pallas kernels  60.5 us (99%)
    pallas_call x1, Pallas kernels, local_product(): pl.pallas_call(gather_kernel, out_shape=tuple((pltpu.VMEM((BLOCK, EARLY),...  39.9 us
    pallas_call x1, Pallas kernels, local_product(): pl.pallas_call(finish_kernel, out_shape=(jax.ShapeDtypeStruct((order, wid...  20.6 us

profile of v8, /device:TPU:0, one launch (start us, length us, event | category | flops | bytes accessed | tf_op | source)
XLA Modules:
  0.0 60.7 jit_solution(15732099684356090320)
XLA Ops:
  0.0 39.9 %gather_and_multiply.1 = (bf16[256,5632]{1,0:T(8,128)(2,1)S(1)}, bf16[256,5632]{1,0:T(8,128)(2,1)S(1)}, bf16[256,5632]{1,0:T(8,128)(2,1)S(1)}, bf16[256,5632]{1,...) custom-call(bf16[2048,512]{1,0:T(8,128)(2,1)} %l_ref.1, ...), custom_call_target="tpu_custom_call" | custom-call | tf_op jit(solution)/shard_map/gather_and_multiply/pallas_call | solution.py:218
  39.9 20.6 %finish.1 = (bf16[2048,8192]{1,0:T(8,128)(2,1)}, bf16[2048,5632]{1,0:T(8,128)(2,1)S(1)}) custom-call(bf16[256,5632]{1,0:T(8,128)(2,1)S(1)} %get-tuple-element.23.refs_0_, bf16[256,5632]{1,0:T(8,128)(2,1)S(1)} %get-tuple-element.24.refs_1_, bf16[256,5632]{1,0:T(8,128)(2,1)S(1)} %get-tuple-element.25.refs_2_, ...), custom_call_target="tpu_custom_call", output_to_operand_aliasing={{1}: (16, {})} | custom-call | tf_op jit(solution)/shard_map/finish/pallas_call | solution.py:273

commit v9 on v7

--- a/solution.py
+++ b/solution.py
@@ -71,7 +71,20 @@
                 return l_ref.at[pl.ds(row * BLOCK, BLOCK), pl.ds(t * BLOCK, BLOCK)]
 
             def own_copy(row, t):
-                return pltpu.make_async_copy(mine(row, t), panel(row, me, t), own_sem.at[row, t])
+                return pltpu.make_async_copy(mine(row, t), panel(row, me, t), own_sem)
+
+            def slot(row, t, part=0):
+                if part:
+                    return 2 * n_rows - group + row
+                return row if t == 0 else n_rows - group + row
+
+            def wait_all(sem, owner, halves):
+                for c in range(group):
+                    width = (2 * n_rows - group - 2 * c) * BLOCK - (BLOCK // 2 if halves else 0)
+                    like = x_refs[last].at[:, pl.ds(0, width)]
+                    pl.when(owner == c)(lambda like=like: pltpu.make_async_copy(like, like, sem).wait())
+
+            last = n_rows - 1
 
             def remote(src, dst, send_sem, recv_sem, peer):
                 return pltpu.make_async_remote_copy(
@@ -79,7 +92,7 @@
 
             def share(row, t, owner):
                 block = panel(row, owner, t)
-                return remote(block, block, p_send.at[row, t], p_recv.at[row, t], partner)
+                return remote(block, block, p_send, p_recv.at[slot(row, t)], partner)
 
             def parts(row, t, owner, send_sem, recv_sem, peer, act):
                 for cond, rects in pieces(row, t, owner):
@@ -87,7 +100,7 @@
                         for j, (first, rows, width) in enumerate(rects):
                             start = pl.multiple_of((owner + group * t) * BLOCK, BLOCK)
                             part = l_refs[row].at[pl.ds(first, rows), pl.ds(start, width)]
-                            act(j, remote(part, part, send_sem.at[row, t, j], recv_sem.at[row, t, j], peer))
+                            act(j, remote(part, part, send_sem, recv_sem.at[slot(row, t, j)], peer))
                     when(cond, run)
 
             def parts_both(row, t, owner, act):
@@ -96,25 +109,28 @@
                         for j, (first, rows, width) in enumerate(rects):
                             start = pl.multiple_of((owner + group * t) * BLOCK, BLOCK)
                             part = l_refs[row].at[pl.ds(first, rows), pl.ds(start, width)]
-                            act(remote(part, part, x_send.at[row, t, j], x_recv.at[row, t, j], across),
-                                remote(part, part, f_send.at[row, t, j], f_recv.at[row, t, j], partner))
+                            act(remote(part, part, x_send, x_recv.at[slot(row, t, j)], across),
+                                remote(part, part, f_send, f_recv.at[slot(row, t, j)], partner))
                     when(cond, run)
 
             near = me - lax.rem(me, 2)
             far = 2 - near
 
-            def load_b(k):
+            def load_b(k, sem):
                 rows = pl.ds(pl.multiple_of(k * BLOCK, BLOCK), BLOCK)
-                return pltpu.make_async_copy(b_ref.at[rows, pl.ds(0, EARLY)], b_vmem.at[rows, :], b_sem.at[k])
+                return pltpu.make_async_copy(b_ref.at[rows, pl.ds(0, EARLY)], b_vmem.at[rows, :], sem)
+
+            def wait_side(i):
+                like = b_vmem.at[pl.ds(0, n_rows // 2 * BLOCK), :]
+                pltpu.make_async_copy(like, like, b_sem.at[i]).wait()
 
             def load_late(k):
                 rows, start = late_place(k)
                 return pltpu.make_async_copy(
-                    b_ref.at[pl.ds(k * BLOCK, BLOCK), pl.ds(EARLY, late)], b_vmem.at[rows, pl.ds(start, late)], late_sem.at[k])
+                    b_ref.at[pl.ds(k * BLOCK, BLOCK), pl.ds(EARLY, late)], b_vmem.at[rows, pl.ds(start, late)], late_sem)
 
             sequence = [3, 6, 5, 4, 7, 2, 1, 0]
             before = [8, 8, 8, 8, 5, 5, 0, 0]
-            last = n_rows - 1
             blocks = [(row, t) for row in sequence for t in range(per_dev)]
             shared = [(last, t) for t in range(per_dev)] + [b for b in blocks if b[0] != last]
 
@@ -127,12 +143,11 @@
                 def clear(row=row):
                     l_refs[row][:BLOCK // 2, row * BLOCK + BLOCK // 2:] = jnp.zeros((BLOCK // 2, BLOCK // 2), dtype)
                 when(far == row % group // 2 * 2, clear)
-            for row, t in shared:
-                when(held(row, me, t), lambda row=row, t=t: own_copy(row, t).wait())
-            for side in (near, far):
+            wait_all(own_sem, me, False)
+            for i, side in enumerate((near, far)):
                 for t in range(per_dev):
                     for c in range(2):
-                        load_b(side + group * t + c).start()
+                        load_b(side + group * t + c, b_sem.at[i]).start()
             pl.semaphore_wait(barrier, 2)
 
             for row, t in blocks:
@@ -170,17 +185,13 @@
                     preferred_element_type=jnp.float32).astype(dtype)
 
             wait_near(last)
-            for t in range(per_dev):
-                for c in range(2):
-                    load_b(near + group * t + c).wait()
+            wait_side(0)
             middle = EARLY // (2 * TILE) * TILE
             for start in range(0, EARLY, TILE):
                 if start == middle:
                     relay(sequence[0])
                 partial[:, start:start + TILE] = half_product(near, start, start + TILE)
-            for t in range(per_dev):
-                for c in range(2):
-                    load_b(far + group * t + c).wait()
+            wait_side(1)
 
             freed = []
             for place, row in enumerate(sequence):
@@ -201,12 +212,11 @@
                         for piece in range(2 * (last - k), 2 * (n_rows - k)):
                             load_late(piece).start()
 
-            for k in range(n_rows):
-                load_late(k).wait()
-            for row, t in blocks:
-                parts(row, t, me, x_send, x_recv, across, lambda j, copy: copy.wait_send())
-                when(held(row, me, t), lambda row=row, t=t: share(row, t, me).wait_send())
-                parts(row, t, across, f_send, f_recv, partner, lambda j, copy: copy.wait_send())
+            like = b_vmem.at[:, pl.ds(0, late)]
+            pltpu.make_async_copy(like, like, late_sem).wait()
+            wait_all(x_send, me, True)
+            wait_all(p_send, me, False)
+            wait_all(f_send, across, True)
 
         dma = pltpu.SemaphoreType.DMA
         vmem = pl.BlockSpec(memory_space=pltpu.VMEM)
@@ -218,8 +228,8 @@
             + (pltpu.VMEM((order, EARLY), dtype),),
             in_specs=[hbm, hbm],
             out_specs=(vmem,) * (2 * n_rows + 1),
-            scratch_shapes=[pltpu.VMEM((BLOCK, EARLY), jnp.float32), dma((n_rows,)), dma((n_rows,))]
-            + [dma((n_rows, per_dev))] * 3 + [dma((n_rows, per_dev, 2))] * 4,
+            scratch_shapes=[pltpu.VMEM((BLOCK, EARLY), jnp.float32), dma((2,)), dma, dma,
+                            dma, dma((2 * n_rows - group,)), dma, dma((3 * n_rows - group,)), dma, dma((3 * n_rows - group,))],
             compiler_params=pltpu.CompilerParams(
                 collective_id=0, has_side_effects=True, vmem_limit_bytes=8 * MIB),
             name="gather_and_multiply",
@@ -231,13 +241,17 @@
 
             def put_early(row):
                 return pltpu.make_async_copy(
-                    x_refs[row], out_ref.at[pl.ds(row * BLOCK, BLOCK), pl.ds(0, EARLY)], early_sem.at[row])
+                    x_refs[row], out_ref.at[pl.ds(row * BLOCK, BLOCK), pl.ds(0, EARLY)], early_sem)
 
             def put_late(n, row):
                 rows = pl.ds(row * BLOCK, BLOCK)
                 cols = pl.ds(EARLY + n * TILE, TILE)
                 slot = n % 2
-                return pltpu.make_async_copy(x_vmem.at[slot, rows, :], out_ref.at[rows, cols], x_sem.at[slot, row])
+                return pltpu.make_async_copy(x_vmem.at[slot, rows, :], out_ref.at[rows, cols], x_sem.at[slot])
+
+            def wait_tile(n):
+                like = x_vmem.at[n % 2]
+                pltpu.make_async_copy(like, like, x_sem.at[n % 2]).wait()
 
             for row in range(n_rows - 1, 4, -1):
                 put_early(row).start()
@@ -247,8 +261,7 @@
                     if n == 1 + row // 2:
                         put_early(row).start()
                 if n >= 2:
-                    for row in range(n_rows):
-                        put_late(n - 2, row).wait()
+                    wait_tile(n - 2)
                 for row in range(n_rows - 1, -1, -1):
                     total = None
                     for k in range(row + 1):
@@ -260,18 +273,17 @@
                     x_vmem[n % 2, row * BLOCK:(row + 1) * BLOCK, :] = total.astype(dtype)
                     put_late(n, row).start()
 
-            for row in range(n_rows):
-                put_early(row).wait()
+            like = b_vmem
+            pltpu.make_async_copy(like, like, early_sem).wait()
             for n in range(n_late - 2, n_late):
-                for row in range(n_rows):
-                    put_late(n, row).wait()
+                wait_tile(n)
 
         return pl.pallas_call(
             finish_kernel,
             out_shape=jax.ShapeDtypeStruct((order, width), dtype),
             in_specs=[vmem] * (2 * n_rows + 1),
             out_specs=hbm,
-            scratch_shapes=[pltpu.VMEM((2, order, TILE), dtype), dma((2, n_rows)), dma((n_rows,))],
+            scratch_shapes=[pltpu.VMEM((2, order, TILE), dtype), dma((2,)), dma],
             compiler_params=pltpu.CompilerParams(vmem_limit_bytes=5 * MIB),
             name="finish",
         )(*gathered)

time: 54.4 us -> 52.9 us (0.972)
  Pallas kernels: 54 us -> 52.5 us
    pallas_call x1, Pallas kernels: 39.9 us -> 38.6 us  [local_product(): pl.pallas_call(gather_kernel, out_shape=tuple((pltpu.VMEM((BLOCK, EARLY),...]
where the time goes in v9:
time: 52.9 us; the launch traced here: 52.7 us
  Pallas kernels  52.5 us (99%)
    pallas_call x1, Pallas kernels, local_product(): pl.pallas_call(gather_kernel, out_shape=tuple((pltpu.VMEM((BLOCK, EARLY),...  38.6 us
    pallas_call x1, Pallas kernels, local_product(): pl.pallas_call(finish_kernel, out_shape=jax.ShapeDtypeStruct((order, widt...  13.9 us

profile of v9, /device:TPU:0, one launch (start us, length us, event | category | flops | bytes accessed | tf_op | source)
XLA Modules:
  0.0 52.7 jit_solution(16120455264759138779)
XLA Ops:
  0.0 38.6 %gather_and_multiply.1 = (bf16[256,5632]{1,0:T(8,128)(2,1)S(1)}, bf16[256,5632]{1,0:T(8,128)(2,1)S(1)}, bf16[256,5632]{1,0:T(8,128)(2,1)S(1)}, bf16[256,5632]{1,...) custom-call(bf16[2048,512]{1,0:T(8,128)(2,1)} %l_ref.1, ...), custom_call_target="tpu_custom_call" | custom-call | tf_op jit(solution)/shard_map/gather_and_multiply/pallas_call | solution.py:224
  38.7 13.9 %finish.1 = bf16[2048,8192]{1,0:T(8,128)(2,1)} custom-call(bf16[256,5632]{1,0:T(8,128)(2,1)S(1)} %get-tuple-element.22.refs_0_, bf16[256,5632]{1,0:T(8,128)(2,1)S(1)} %get-tuple-element.23.refs_1_, bf16[256,5632]{1,0:T(8,128)(2,1)S(1)} %get-tuple-element.24.refs_2_, bf16[256,5632]{1,0:T(8,128)(2,1)S(1)} %get-tuple-element.25.refs_3_, ...), custom_call_target="tpu_custom_call" | custom-call | tf_op jit(solution)/shard_map/finish/pallas_call | solution.py:281

commit v10 on v9

--- a/solution.py
+++ b/solution.py
@@ -73,17 +73,20 @@
             def own_copy(row, t):
                 return pltpu.make_async_copy(mine(row, t), panel(row, me, t), own_sem)
 
-            def slot(row, t, part=0):
-                if part:
-                    return 2 * n_rows - group + row
-                return row if t == 0 else n_rows - group + row
-
             def wait_all(sem, owner, halves):
                 for c in range(group):
                     width = (2 * n_rows - group - 2 * c) * BLOCK - (BLOCK // 2 if halves else 0)
                     like = x_refs[last].at[:, pl.ds(0, width)]
                     pl.when(owner == c)(lambda like=like: pltpu.make_async_copy(like, like, sem).wait())
 
+            def wait_row(sem, row, owner):
+                for c in range(group):
+                    size = sum(rows * width for t in range(per_dev) for cond, rects in pieces(row, t, c) if cond
+                               for _, rows, width in rects)
+                    if size:
+                        like = b_vmem.at[pl.ds(0, size // BLOCK), pl.ds(0, BLOCK)]
+                        pl.when(owner == c)(lambda like=like: pltpu.make_async_copy(like, like, sem.at[row]).wait())
+
             last = n_rows - 1
 
             def remote(src, dst, send_sem, recv_sem, peer):
@@ -92,7 +95,7 @@
 
             def share(row, t, owner):
                 block = panel(row, owner, t)
-                return remote(block, block, p_send, p_recv.at[slot(row, t)], partner)
+                return remote(block, block, p_send, p_recv.at[0 if row == last else 1], partner)
 
             def parts(row, t, owner, send_sem, recv_sem, peer, act):
                 for cond, rects in pieces(row, t, owner):
@@ -100,7 +103,7 @@
                         for j, (first, rows, width) in enumerate(rects):
                             start = pl.multiple_of((owner + group * t) * BLOCK, BLOCK)
                             part = l_refs[row].at[pl.ds(first, rows), pl.ds(start, width)]
-                            act(j, remote(part, part, send_sem, recv_sem.at[slot(row, t, j)], peer))
+                            act(j, remote(part, part, send_sem, recv_sem.at[row], peer))
                     when(cond, run)
 
             def parts_both(row, t, owner, act):
@@ -109,8 +112,7 @@
                         for j, (first, rows, width) in enumerate(rects):
                             start = pl.multiple_of((owner + group * t) * BLOCK, BLOCK)
                             part = l_refs[row].at[pl.ds(first, rows), pl.ds(start, width)]
-                            act(remote(part, part, x_send, x_recv.at[slot(row, t, j)], across),
-                                remote(part, part, f_send, f_recv.at[slot(row, t, j)], partner))
+                            act(remote(part, part, f_send, f_recv.at[row], partner))
                     when(cond, run)
 
             near = me - lax.rem(me, 2)
@@ -156,15 +158,15 @@
                 when(held(row, me, t), lambda row=row, t=t: share(row, t, me).start())
 
             def relay(row):
-                def step(came, on):
-                    came.wait_recv()
-                    on.start()
+                wait_row(x_recv, row, across)
                 for t in range(per_dev):
-                    parts_both(row, t, across, step)
-
-            def wait_near(row):
-                for t in range(per_dev):
-                    when(held(row, partner, t), lambda t=t: share(row, t, partner).wait_recv())
+                    parts_both(row, t, across, lambda copy: copy.start())
+
+            def wait_near(rest):
+                for c in range(group):
+                    width = (2 * n_rows - group - 2 * c - per_dev if rest else per_dev) * BLOCK
+                    like = x_refs[last].at[:, pl.ds(0, width)]
+                    pl.when(partner == c)(lambda like=like: pltpu.make_async_copy(like, like, p_recv.at[rest]).wait())
 
             def half_product(side, start, stop):
                 total = None
@@ -184,7 +186,7 @@
                     l_refs[row][...], b_vmem[:(row + 1) * BLOCK, start:stop],
                     preferred_element_type=jnp.float32).astype(dtype)
 
-            wait_near(last)
+            wait_near(0)
             wait_side(0)
             middle = EARLY // (2 * TILE) * TILE
             for start in range(0, EARLY, TILE):
@@ -195,10 +197,9 @@
 
             freed = []
             for place, row in enumerate(sequence):
-                if row != last:
-                    wait_near(row)
-                for t in range(per_dev):
-                    parts(row, t, diagonal, f_send, f_recv, partner, lambda j, copy: copy.wait_recv())
+                if place == 0:
+                    wait_near(1)
+                wait_row(f_recv, row, diagonal)
                 split = before[place] * TILE
                 if split:
                     multiply(row, 0, split)
@@ -229,7 +230,7 @@
             in_specs=[hbm, hbm],
             out_specs=(vmem,) * (2 * n_rows + 1),
             scratch_shapes=[pltpu.VMEM((BLOCK, EARLY), jnp.float32), dma((2,)), dma, dma,
-                            dma, dma((2 * n_rows - group,)), dma, dma((3 * n_rows - group,)), dma, dma((3 * n_rows - group,))],
+                            dma, dma((2,)), dma, dma((n_rows,)), dma, dma((n_rows,))],
             compiler_params=pltpu.CompilerParams(
                 collective_id=0, has_side_effects=True, vmem_limit_bytes=8 * MIB),
             name="gather_and_multiply",

time: 52.9 us -> 52.7 us (level)
  no operation moved by 1% of the time
where the time goes in v10:
time: 52.7 us; the launch traced here: 52.6 us
  Pallas kernels  52.4 us (99%)
    pallas_call x1, Pallas kernels, local_product(): pl.pallas_call(gather_kernel, out_shape=tuple((pltpu.VMEM((BLOCK, EARLY),...  38.6 us
    pallas_call x1, Pallas kernels, local_product(): pl.pallas_call(finish_kernel, out_shape=jax.ShapeDtypeStruct((order, widt...  13.9 us

profile of v10, /device:TPU:0, one launch (start us, length us, event | category | flops | bytes accessed | tf_op | source)
XLA Modules:
  0.0 52.6 jit_solution(5886409354612117518)
XLA Ops:
  0.0 38.6 %gather_and_multiply.1 = (bf16[256,5632]{1,0:T(8,128)(2,1)S(1)}, bf16[256,5632]{1,0:T(8,128)(2,1)S(1)}, bf16[256,5632]{1,0:T(8,128)(2,1)S(1)}, bf16[256,5632]{1,...) custom-call(bf16[2048,512]{1,0:T(8,128)(2,1)} %l_ref.1, ...), custom_call_target="tpu_custom_call" | custom-call | tf_op jit(solution)/shard_map/gather_and_multiply/pallas_call | solution.py:225
  38.6 13.9 %finish.1 = bf16[2048,8192]{1,0:T(8,128)(2,1)} custom-call(bf16[256,5632]{1,0:T(8,128)(2,1)S(1)} %get-tuple-element.22.refs_0_, bf16[256,5632]{1,0:T(8,128)(2,1)S(1)} %get-tuple-element.23.refs_1_, bf16[256,5632]{1,0:T(8,128)(2,1)S(1)} %get-tuple-element.24.refs_2_, bf16[256,5632]{1,0:T(8,128)(2,1)S(1)} %get-tuple-element.25.refs_3_, ...), custom_call_target="tpu_custom_call" | custom-call | tf_op jit(solution)/shard_map/finish/pallas_call | solution.py:282
